TPU v7x, 256 devices: a whole 4x4x8 slice. The times are simulated.
256 devices in a mesh: lon: 16 (over z, y_lo), lat: 16 (over x, y_hi, core).
Axes of the slice: x: 4, y: 4 (y_hi: 2, y_lo: 2; y = y_hi * 2 + y_lo), z: 8, core: 2. Of those that a mesh axis runs over, the one named last changes fastest.
Arguments:
- velocity: bfloat16 [3, 75, 512, 4096], P(None, None, 'lat', 'lon'), may hold values from -1.5 to 1.5
- offsets: float32 [3, 16, 12288], P(None, 'lat', 'lon'), may hold values from 0 to 1
- cells: int32 [3, 16, 12288], P(None, 'lat', 'lon'), may hold values from 0 to 255, as said below
- counts: int32 [16, 16], P('lat', 'lon'), may hold values from 192 to 576, as said below
- moves: int32 [16, 12288], P('lat', 'lon'), may hold values from 0 to 4, as said below
Outputs:
- new_offsets: float32 [3, 16, 12288], P(None, 'lat', 'lon')
- new_cells: int32 [3, 16, 12288], P(None, 'lat', 'lon')
- new_counts: int32 [16, 16], P('lat', 'lon')
Inputs may be any that keep to these rules, and one draw needn't show every extreme that they name: `cells`: values from 0 to 255, 31 and 73 for i, j, k. A valid slot with move 1 has i = 255, move 2 i = 0, move 3 j = 31, move 4 j = 0. `counts`: between 192 and 576; the upper bound is reached by some tile in every draw. `moves`: invalid slots have 0. In each tile at most 48 valid particles have each nonzero move, and in every draw some tile has exactly 48 for each move. Tiles of row 0 have no move 4.
All inputs are finite; a program needn't handle non-finite values.
Results may differ from a plain program's by a relative error of at most 0.00093.
Values may be sent and summed in bfloat16 or wider, within the bound.
A program may use at most 64 MiB of HBM per device.

v0:
```python
import jax
import jax.numpy as jnp
from jax import lax
from jax.sharding import PartitionSpec as P

BLOCK = 256
CAP = 48


def shifted(block, axis, distance):
    devices = range(lax.axis_size(axis))
    route = [((i - distance) % len(devices), i) for i in devices]
    return lax.ppermute(block, axis, route)


def from_behind(x, axis, by):
    count = lax.axis_size(axis)
    pairs = [(i, i + by) for i in range(count) if 0 <= i + by < count]
    return lax.ppermute(x, axis, pairs)


def swapped(block, axis, stride):
    count = lax.axis_size(axis)
    route = []
    for low in range(count):
        high = low | 1 << stride
        if high != low and high < count:
            route += [(low, high), (high, low)]
    return lax.ppermute(block, axis, route)


def extended(cells, sides, width, closed):
    for axis, dim in sides:
        count = lax.axis_size(axis)
        ends = count if closed else count - 1
        head = lax.slice_in_dim(cells, 0, width, axis=dim)
        tail = lax.slice_in_dim(cells, cells.shape[dim] - width, cells.shape[dim], axis=dim)
        cells = jnp.concatenate(
            [
                lax.ppermute(tail, axis, [(i, (i + 1) % count) for i in range(ends)]),
                cells,
                lax.ppermute(head, axis, [((i + 1) % count, i) for i in range(ends)]),
            ],
            axis=dim,
        )
    return cells


def sample(planes, north_main, east_col, corner, position, cellpos):
    a, b, c = (position[0], position[1], position[2])
    col_i, row_j, lev_k = (cellpos[0], cellpos[1], cellpos[2])
    count = position.shape[1]
    depth = north_main.shape[1]
    cols_here = north_main.shape[2]
    plane_rows = planes.shape[1]
    rows_here = plane_rows // depth
    inner = (row_j + 1 < rows_here)[:, None]
    at_edge = (row_j == rows_here - 1)[:, None]
    w_one = ((1.0 - b) * (1.0 - c))[:, None]
    w_two = (b * (1.0 - c))[:, None]
    w_three = ((1.0 - b) * c)[:, None]
    w_four = (b * c)[:, None]
    base = (lev_k * rows_here + row_j)[:, None]
    index = lax.broadcasted_iota(jnp.int32, (count, plane_rows), 1)
    w_main = jnp.where(index == base, w_one, 0.0)
    w_main = w_main + jnp.where((index == base + 1) & inner, w_two, 0.0)
    w_main = w_main + jnp.where(index == base + rows_here, w_three, 0.0)
    w_main = w_main + jnp.where((index == base + rows_here + 1) & inner, w_four, 0.0)
    w_main = w_main.astype(jnp.bfloat16)
    level_index = lax.broadcasted_iota(jnp.int32, (count, depth), 1)
    w_north = jnp.where((level_index == lev_k[:, None]) & at_edge, w_two, 0.0)
    w_north = w_north + jnp.where((level_index == lev_k[:, None] + 1) & at_edge, w_four, 0.0)
    w_north = w_north.astype(jnp.bfloat16)
    column = lax.broadcasted_iota(jnp.int32, (count, cols_here), 1)
    col_weight = jnp.where(column == col_i[:, None], (1.0 - a)[:, None], 0.0)
    col_weight = col_weight + jnp.where(column == (col_i + 1)[:, None], a[:, None], 0.0)
    east_weight = jnp.where(col_i + 1 == cols_here, a, 0.0)
    east_sum = jnp.dot(w_main, east_col.T, preferred_element_type=jnp.float32)
    east_sum = east_sum + jnp.dot(w_north, corner.T, preferred_element_type=jnp.float32)
    parts = []
    for comp in range(3):
        combined = jnp.dot(w_main, planes[comp], preferred_element_type=jnp.float32)
        combined = combined + jnp.dot(w_north, north_main[comp], preferred_element_type=jnp.float32)
        parts.append(jnp.sum(combined * col_weight, axis=1) + east_weight * east_sum[:, comp])
    return jnp.stack(parts)


def compact(records, selected, size):
    chosen = selected.astype(jnp.int32)
    place = jnp.where(selected, jnp.cumsum(chosen) - chosen, size)
    target = lax.broadcasted_iota(jnp.int32, (records.shape[1], size), 1)
    placing = (place[:, None] == target).astype(jnp.float32)
    return jnp.dot(records, placing, precision=lax.Precision.HIGHEST)


def shards(velocity, offsets, cells, counts, moves):
    depth, rows_here, cols_here = (velocity.shape[1], velocity.shape[2], velocity.shape[3])
    slots = offsets.shape[2]
    lat_size = lax.axis_size("lat")
    lon_size = lax.axis_size("lon")
    lat_index = lax.axis_index("lat")
    is_top = lat_index == lat_size - 1
    bits = lon_size.bit_length() - 1
    east = shifted(velocity[:, :, :, :1], "lon", -1)
    edge_row = jnp.concatenate([velocity[:, :, :1, :], east[:, :, :1, :]], axis=3)
    above = from_behind(edge_row, "lat", -1)
    top_row = jnp.concatenate(
        [velocity[:, :, rows_here - 1 :, :], east[:, :, rows_here - 1 :, :]], axis=3
    )
    mirrored = top_row
    for bit in range(bits):
        mirrored = swapped(mirrored, "lon", bit)
    ghost = -jnp.flip(mirrored, axis=3)
    northern = jnp.where(is_top, ghost, above)
    north_main = northern[:, :, 0, :cols_here]
    corner = northern[:, :, 0, cols_here]
    east_col = east[:, :, :, 0].reshape(3, depth * rows_here)
    planes = velocity.reshape(3, depth * rows_here, cols_here)
    position = offsets[:, 0, :]
    cellpos = cells[:, 0, :]
    live_count = counts[0, 0]
    blocks = (live_count + BLOCK - 1) // BLOCK

    def advance(step, result):
        start = step * BLOCK
        pos = lax.dynamic_slice_in_dim(position, start, BLOCK, 1)
        cel = lax.dynamic_slice_in_dim(cellpos, start, BLOCK, 1)
        first = sample(planes, north_main, east_col, corner, pos, cel)
        second = sample(planes, north_main, east_col, corner, pos + 0.5 * first, cel)
        return lax.dynamic_update_slice_in_dim(result, pos + second, start, 1)

    moved = lax.fori_loop(0, blocks, advance, jnp.zeros((3, slots), jnp.float32))
    slot_index = jnp.arange(slots, dtype=jnp.int32)
    valid = slot_index < live_count
    motion = moves[0]
    col_i, row_j, lev_k = (cellpos[0], cellpos[1], cellpos[2])
    na, nb, nc = (moved[0], moved[1], moved[2])
    folding = (motion == 3) & is_top
    new_a = jnp.where(
        motion == 1, na - 1.0, jnp.where(motion == 2, na + 1.0, jnp.where(folding, 1.0 - na, na))
    )
    new_b = jnp.where(
        motion == 3, jnp.where(is_top, 2.0 - nb, nb - 1.0), jnp.where(motion == 4, nb + 1.0, nb)
    )
    new_i = jnp.where(
        motion == 1,
        0,
        jnp.where(motion == 2, cols_here - 1, jnp.where(folding, cols_here - 1 - col_i, col_i)),
    )
    new_j = jnp.where(
        motion == 3,
        jnp.where(is_top, rows_here - 1, 0),
        jnp.where(motion == 4, rows_here - 1, row_j),
    )
    code = (1 + new_i + cols_here * (new_j + rows_here * lev_k)).astype(jnp.float32)
    records = jnp.stack([new_a, new_b, nc, code])
    staying = compact(records, valid & (motion == 0), slots)
    stay_count = jnp.sum((valid & (motion == 0)).astype(jnp.int32))
    east_going = compact(records, valid & (motion == 1), CAP)
    west_going = compact(records, valid & (motion == 2), CAP)
    north_going = compact(records, valid & (motion == 3), CAP)
    south_going = compact(records, valid & (motion == 4), CAP)
    lon_side = extended(jnp.stack([west_going, east_going], axis=1), (("lon", 1),), 1, True)
    lat_side = extended(jnp.stack([south_going, north_going], axis=1), (("lat", 1),), 1, False)
    folded = north_going
    for bit in range(bits):
        folded = swapped(folded, "lon", bit)
    folded = jnp.where(is_top, folded, 0.0)
    arrivals = [lon_side[:, 0], lon_side[:, 3], lat_side[:, 0], lat_side[:, 3], folded]
    output = staying
    filled = stay_count
    lane = jnp.arange(CAP, dtype=jnp.int32)
    target = lax.broadcasted_iota(jnp.int32, (CAP, slots), 1)
    for parcel in arrivals:
        present = parcel[3] > 0.5
        place = jnp.where(present, filled + lane, slots)
        placing = (place[:, None] == target).astype(jnp.float32)
        output = output + jnp.dot(parcel, placing, precision=lax.Precision.HIGHEST)
        filled = filled + jnp.sum(present.astype(jnp.int32))
    decoded = jnp.maximum(output[3].astype(jnp.int32) - 1, 0)
    out_i = decoded % cols_here
    out_j = decoded // cols_here % rows_here
    out_k = decoded // (cols_here * rows_here)
    new_offsets = output[:3][:, None, :]
    new_cells = jnp.stack([out_i, out_j, out_k])[:, None, :]
    return (new_offsets, new_cells, filled.reshape(1, 1))


def solution(mesh):
    placed = (
        P(None, None, "lat", "lon"),
        P(None, "lat", "lon"),
        P(None, "lat", "lon"),
        P("lat", "lon"),
        P("lat", "lon"),
    )
    return jax.shard_map(
        shards,
        mesh=mesh,
        in_specs=placed,
        out_specs=(P(None, "lat", "lon"), P(None, "lat", "lon"), P("lat", "lon")),
        check_vma=False,
    )
```

profile of v0, /device:TPU:4, one launch (start us, length us, event | category | flops | bytes accessed | tf_op | source)
XLA Modules:
  0.0 154.9 jit_solution(8371439635145533388)
XLA Ops:
  0.7 1.5 slice-done
  2.1 1.7 %copy.36 = bf16[3,75,32,1]{1,2,3,0:T(8,128)(2,1)S(1)} copy(bf16[3,75,32,1]{3,2,1,0:T(8,128)(2,1)S(1)} %slice-done) | data formatting | bytes 28800
  3.9 6.9 %collective-permute-start = (bf16[3,75,32,1]{1,2,3,0:T(8,128)(2,1)S(1)}, bf16[3,75,32,1]{1,2,3,0:T(8,128)(2,1)S(1)}, u32[]{:S(2)}, u32[]{:S(2)}) collective-permute-start(bf16[3,75,32,1]{1,2,3,0:T(8,128)(2,1)S(1)} %copy.36), channel_id=1, source_target_pairs={{16,0},{32,16},{48,32},{64,48},{80,64},{96,80},{112,96},{128,112},... | collective-permute-start | bytes 43208 | tf_op jit(solution)/shard_map/ppermute | solution.py:13
  10.8 1.8 %fusion.174 = (bf16[3,75,1,256]{3,2,1,0:T(2,128)(2,1)S(1)}, bf16[3,75,1,256]{3,2,1,0:T(2,128)(2,1)S(1)}) fusion(bf16[3,75,32,256]{3,2,1,0:T(8,128)(2,1)} %param.7), kind=kLoop, calls=%fused_computation.255 | loop fusion | bytes 460800 | tf_op jit(solution)/shard_map/slice | solution.py:108
  15.6 0.7 fusion.134
  17.3 5.5 %collective-permute-done.1 = bf16[3,75,1,257]{3,1,0,2:T(8,128)(2,1)S(1)} collective-permute-done((bf16[3,75,1,257]{3,1,0,2:T(8,128)(2,1)S(1)}, bf16[3,75,1,257]{3,1,0,2:T(8,128)(2,1)S(1)}, u32[]{:S(2)}, u32[]{:S(2)}) %collective-permute-start.1) | collective-permute-done | bytes 115682 | tf_op jit(solution)/shard_map/ppermute | solution.py:29
  23.0 5.3 %collective-permute-done.2 = bf16[3,75,1,257]{3,1,0,2:T(8,128)(2,1)S(1)} collective-permute-done((bf16[3,75,1,257]{3,1,0,2:T(8,128)(2,1)S(1)}, bf16[3,75,1,257]{3,1,0,2:T(8,128)(2,1)S(1)}, u32[]{:S(2)}, u32[]{:S(2)}) %collective-permute-start.2) | collective-permute-done | bytes 115682 | tf_op jit(solution)/shard_map/ppermute | solution.py:29
  28.3 1.9 %collective-permute-start.5 = (bf16[3,75,1,257]{3,1,0,2:T(8,128)(2,1)S(1)}, bf16[3,75,1,257]{3,1,0,2:T(8,128)(2,1)S(1)}, u32[]{:S(2)}, u32[]{:S(2)}) collective-permute-start(bf16[3,75,1,257]{3,1,0,2:T(8,128)(2,1)S(1)} %pad_maximum_fusion.1), channel_id=1, source_target_pairs={{1,0},{2,1},{3,2},{4,3},{5,4},{6,5},{7,6},{8,7},{9,8},{10,9},{11,1... | collective-permute-start | bytes 346958 | tf_op jit(solution)/shard_map/ppermute | solution.py:19
  30.3 6.7 %collective-permute-done.3 = bf16[3,75,1,257]{3,1,0,2:T(8,128)(2,1)S(1)} collective-permute-done((bf16[3,75,1,257]{3,1,0,2:T(8,128)(2,1)S(1)}, bf16[3,75,1,257]{3,1,0,2:T(8,128)(2,1)S(1)}, u32[]{:S(2)}, u32[]{:S(2)}) %collective-permute-start.3) | collective-permute-done | bytes 115682 | tf_op jit(solution)/shard_map/ppermute | solution.py:29
  36.9 2.0 %collective-permute-start.4 = (bf16[3,75,1,257]{3,1,0,2:T(8,128)(2,1)S(1)}, bf16[3,75,1,257]{3,1,0,2:T(8,128)(2,1)S(1)}, u32[]{:S(2)}, u32[]{:S(2)}) collective-permute-start(bf16[3,75,1,257]{3,1,0,2:T(8,128)(2,1)S(1)} %collective-permute-done.3), channel_id=1, source_target_pairs={{0,128},{128,0},{16,144},{144,16},{32,160},{160,32},{48,176},{176,... | collective-permute-start | bytes 346958 | tf_op jit(solution)/shard_map/ppermute | solution.py:29
  39.2 9.0 %collective-permute-done.4 = bf16[3,75,1,257]{3,1,0,2:T(8,128)(2,1)S(1)} collective-permute-done((bf16[3,75,1,257]{3,1,0,2:T(8,128)(2,1)S(1)}, bf16[3,75,1,257]{3,1,0,2:T(8,128)(2,1)S(1)}, u32[]{:S(2)}, u32[]{:S(2)}) %collective-permute-start.4) | collective-permute-done | bytes 115682 | tf_op jit(solution)/shard_map/ppermute | solution.py:29
  48.3 0.8 reverse
  49.3 23.1 %while.12 = (s32[]{:T(128)}, f32[3,768]{1,0:T(4,128)S(1)}, s32[]{:T(128)}, f32[3,768]{1,0:T(4,128)S(1)}, s32[3,768]{1,0:T(4,128)S(1)}, /*index=5*/bf16[3,2400,25...) while((s32[]{:T(128)}, f32[3,768]{1,0:T(4,128)S(1)}, ...), condition=%wide.region_7.8_spmd, body=%wide.region_0.7_spmd.sunk | while | flops 2027225856 | bytes 25783828 | solution.py:132
  50.2 3.6 %fusion.236 = f32[256]{0:T(256)S(1)} fusion(f32[256,256]{0,1:T(8,128)S(1)} %fusion.235, bf16[3,2400,256]{2,1,0:T(8,128)(2,1)} %get-tuple-element.364, f32[256]{0:T(256)S(1)} %bitcast.333, s32[256]{0:T(256)S(1)} %get-tuple-element.307, f32[256]{0:T(256)S(1)} %get-tuple-element.308, s32[256]{0:T(256)S(1)} %bitcast.323, ...), kind=kOutput, calls=%fused_computation.33.clone.1 | convolution fusion | flops 323698432 | bytes 1504512 | tf_op jit(solution)/shard_map/while/body/dot_general | solution.py:82
  54.2 2.2 %fusion.238 = f32[256]{0:T(256)S(1)} fusion(f32[256,256]{0,1:T(8,128)S(1)} %fusion.237, bf16[3,2400,256]{2,1,0:T(8,128)(2,1)S(1)} %copy-done, f32[256]{0:T(256)S(1)} %bitcast.334, s32[256]{0:T(256)S(1)} %get-tuple-element.307, f32[256]{0:T(256)S(1)} %get-tuple-element.308, s32[256]{0:T(256)S(1)} %bitcast.324, f32[256]{0:T(256)S(1)} %get-tuple-element.300, ...), kind=kOutput, calls=%fused_computation.35.clone.1 | convolution fusion | flops 323698432 | bytes 1504768 | tf_op jit(solution)/shard_map/while/body/dot_general | solution.py:82
  56.9 2.2 %fusion.233 = f32[256]{0:T(256)S(1)} fusion(f32[256,256]{0,1:T(8,128)S(1)} %fusion.232, bf16[3,2400,256]{2,1,0:T(8,128)(2,1)S(1)} %copy-done, f32[256]{0:T(256)S(1)} %bitcast.335, s32[256]{0:T(256)S(1)} %get-tuple-element.307, f32[256]{0:T(256)S(1)} %get-tuple-element.308, s32[256]{0:T(256)S(1)} %bitcast.325, f32[256]{0:T(256)S(1)} %get-tuple-element.300, ...), kind=kOutput, calls=%fused_computation.37.clone.1 | convolution fusion | flops 323698432 | bytes 1504768 | tf_op jit(solution)/shard_map/while/body/dot_general | solution.py:82
  59.1 2.1 %fusion.234 = f32[256,3]{0,1:T(4,128)S(1)} fusion(bf16[3,2400]{1,0:T(4,128)(2,1)S(1)} %get-tuple-element.366, f32[256]{0:T(256)S(1)} %get-tuple-element.300, s32[256]{0:T(256)S(1)} %get-tuple-element.310, f32[256]{0:T(256)S(1)} %get-tuple-element.311, s32[256]{0:T(256)S(1)} %get-tuple-element.312, f32[256]{0:T(256)S(1)} %get-tuple-element.305, ...), kind=kOutput, calls=%fused_computation.124.clone.1 | convolution fusion | flops 12288000 | bytes 25920 | tf_op jit(solution)/shard_map/while/body/dot_general | solution.py:78
  62.1 2.2 %fusion.248 = f32[256]{0:T(256)S(1)} fusion(f32[256,256]{0,1:T(8,128)S(1)} %fusion.247, bf16[3,2400,256]{2,1,0:T(8,128)(2,1)S(1)} %copy-done, f32[256]{0:T(256)S(1)} %bitcast.347, f32[256]{0:T(256)S(1)} %broadcast_subtract_fusion.3, s32[256]{0:T(256)S(1)} %get-tuple-element.307, s32[256]{0:T(256)S(1)} %bitcast.326, f32[256]{0:T(256)S(1)} %get-tuple-element.321, ...), kind=kOutput, calls=%fused_computation.34.clone.1 | convolution fusion | flops 323698432 | bytes 1504768 | tf_op jit(solution)/shard_map/while/body/dot_general | solution.py:82
  64.8 2.2 %fusion.246 = f32[256]{0:T(256)S(1)} fusion(f32[256,256]{0,1:T(8,128)S(1)} %fusion.245, bf16[3,2400,256]{2,1,0:T(8,128)(2,1)S(1)} %copy-done, f32[256]{0:T(256)S(1)} %bitcast.348, f32[256]{0:T(256)S(1)} %broadcast_subtract_fusion.3, s32[256]{0:T(256)S(1)} %get-tuple-element.307, s32[256]{0:T(256)S(1)} %bitcast.327, f32[256]{0:T(256)S(1)} %get-tuple-element.321, ...), kind=kOutput, calls=%fused_computation.32.clone.1 | convolution fusion | flops 323698432 | bytes 1504768 | tf_op jit(solution)/shard_map/while/body/dot_general | solution.py:82
  67.0 2.1 %fusion.244 = f32[256,3]{0,1:T(4,128)S(1)} fusion(bf16[3,2400]{1,0:T(4,128)(2,1)S(1)} %get-tuple-element.366, f32[256]{0:T(256)S(1)} %get-tuple-element.321, f32[256]{0:T(256)S(1)} %get-tuple-element.324, f32[256]{0:T(256)S(1)} %get-tuple-element.322, f32[256]{0:T(256)S(1)} %get-tuple-element.325, s32[256]{0:T(256)S(1)} %get-tuple-element.310, ...), kind=kOutput, calls=%fused_computation.125.clone.1 | convolution fusion | flops 12288000 | bytes 25920 | tf_op jit(solution)/shard_map/while/body/dot_general | solution.py:78
  69.9 2.2 %fusion.243 = f32[256]{0:T(256)S(1)} fusion(f32[256,256]{0,1:T(8,128)S(1)} %fusion.242, bf16[3,2400,256]{2,1,0:T(8,128)(2,1)S(1)} %copy-done, f32[256]{0:T(256)S(1)} %bitcast.349, f32[256]{0:T(256)S(1)} %broadcast_subtract_fusion.3, s32[256]{0:T(256)S(1)} %get-tuple-element.307, s32[256]{0:T(256)S(1)} %bitcast.328, f32[256]{0:T(256)S(1)} %get-tuple-element.321, ...), kind=kOutput, calls=%fused_computation.36.clone.1 | convolution fusion | flops 323698432 | bytes 1504768 | tf_op jit(solution)/shard_map/while/body/dot_general | solution.py:82
  72.8 24.0 %collective-permute-start.10 = (f32[4,48]{1,0:T(4,128)S(1)}, f32[4,48]{1,0:T(4,128)S(1)}, u32[]{:S(2)}, u32[]{:S(2)}) collective-permute-start(f32[4,48]{1,0:T(4,128)S(1)} %fusion.122), channel_id=1, source_target_pairs={{0,16},{16,0},{32,48},{48,32},{64,80},{80,64},{96,112},{112,96},{1... | collective-permute-start | bytes 2312 | tf_op jit(solution)/shard_map/ppermute | solution.py:29
  96.8 23.2 %collective-permute-start.8 = (f32[4,1,48]{2,0,1:T(4,128)S(1)}, f32[4,1,48]{2,0,1:T(4,128)S(1)}, u32[]{:S(2)}, u32[]{:S(2)}) collective-permute-start(f32[4,1,48]{2,0,1:T(4,128)S(1)} %bitcast.361), channel_id=1, source_target_pairs={{0,1},{1,2},{2,3},{3,4},{4,5},{5,6},{6,7},{7,8},{8,9},{9,10},{10,1... | collective-permute-start | bytes 2312 | tf_op jit(solution)/shard_map/ppermute | solution.py:40
  120.3 3.0 %collective-permute-start.7 = (f32[4,1,48]{2,0,1:T(4,128)S(1)}, f32[4,1,48]{2,0,1:T(4,128)S(1)}, u32[]{:S(2)}, u32[]{:S(2)}) collective-permute-start(f32[4,1,48]{2,0,1:T(4,128)S(1)} %convolution_bitcast_fusion.1), channel_id=1, source_target_pairs={{16,0},{32,16},{48,32},{64,48},{80,64},{96,80},{112,96},{128,112},... | collective-permute-start | bytes 2312 | tf_op jit(solution)/shard_map/ppermute | solution.py:42
  124.0 6.4 %collective-permute-start.9 = (f32[4,1,48]{2,0,1:T(4,128)S(1)}, f32[4,1,48]{2,0,1:T(4,128)S(1)}, u32[]{:S(2)}, u32[]{:S(2)}) collective-permute-start(f32[4,1,48]{2,0,1:T(4,128)S(1)} %convolution_bitcast_fusion), channel_id=1, source_target_pairs={{1,0},{2,1},{3,2},{4,3},{5,4},{6,5},{7,6},{8,7},{9,8},{10,9},{11,1... | collective-permute-start | bytes 2312 | tf_op jit(solution)/shard_map/ppermute | solution.py:42
  130.4 0.9 fusion.118
  131.3 1.3 bitcast_select_fusion.5
  137.8 1.2 collective-permute-done.11
  139.2 4.3 %collective-permute-done.12 = f32[4,48]{1,0:T(4,128)S(1)} collective-permute-done((f32[4,48]{1,0:T(4,128)S(1)}, f32[4,48]{1,0:T(4,128)S(1)}, u32[]{:S(2)}, u32[]{:S(2)}) %collective-permute-start.12) | collective-permute-done | bytes 800 | tf_op jit(solution)/shard_map/ppermute | solution.py:29
  143.5 1.4 collective-permute-start.13
  145.7 5.2 %collective-permute-done.13 = f32[4,48]{1,0:T(4,128)S(1)} collective-permute-done((f32[4,48]{1,0:T(4,128)S(1)}, f32[4,48]{1,0:T(4,128)S(1)}, u32[]{:S(2)}, u32[]{:S(2)}) %collective-permute-start.13) | collective-permute-done | bytes 800 | tf_op jit(solution)/shard_map/ppermute | solution.py:29
  151.0 0.6 fusion.171
  (108 shorter events, 13.1 us)
Async XLA Ops:
  0.6 1.5 slice-start
  0.6 12.6 %copy-start.2 = (s32[1,768]{1,0:T(1,128)S(1)}, s32[1,768]{1,0:T(1,128)}, u32[]{:S(2)}) copy-start(s32[1,768]{1,0:T(1,128)} %param.11) | copy-start | bytes 9220
  2.1 14.6 %copy-start.1 = (s32[3,1,768]{2,1,0:T(1,128)S(1)}, s32[3,1,768]{2,1,0:T(1,128)}, u32[]{:S(2)}) copy-start(s32[3,1,768]{2,1,0:T(1,128)} %param.9) | copy-start | bytes 27652
  2.1 14.6 %copy-start.3 = (f32[3,1,768]{2,1,0:T(1,128)S(1)}, f32[3,1,768]{2,1,0:T(1,128)}, u32[]{:S(2)}) copy-start(f32[3,1,768]{2,1,0:T(1,128)} %param.8) | copy-start | bytes 27652
  3.9 12.5 %collective-permute-start = (bf16[3,75,32,1]{1,2,3,0:T(8,128)(2,1)S(1)}, bf16[3,75,32,1]{1,2,3,0:T(8,128)(2,1)S(1)}, u32[]{:S(2)}, u32[]{:S(2)}) collective-permute-start(bf16[3,75,32,1]{1,2,3,0:T(8,128)(2,1)S(1)} %copy.36), channel_id=1, source_target_pairs={{16,0},{32,16},{48,32},{64,48},{80,64},{96,80},{112,96},{128,112},... | collective-permute-start | bytes 43208 | tf_op jit(solution)/shard_map/ppermute | solution.py:13
  16.6 6.2 %collective-permute-start.1 = (bf16[3,75,1,257]{3,1,0,2:T(8,128)(2,1)S(1)}, bf16[3,75,1,257]{3,1,0,2:T(8,128)(2,1)S(1)}, u32[]{:S(2)}, u32[]{:S(2)}) collective-permute-start(bf16[3,75,1,257]{3,1,0,2:T(8,128)(2,1)S(1)} %pad_maximum_fusion), channel_id=1, source_target_pairs={{0,16},{16,0},{32,48},{48,32},{64,80},{80,64},{96,112},{112,96},{1... | collective-permute-start | bytes 346958 | tf_op jit(solution)/shard_map/ppermute | solution.py:29
  22.7 5.5 %collective-permute-start.2 = (bf16[3,75,1,257]{3,1,0,2:T(8,128)(2,1)S(1)}, bf16[3,75,1,257]{3,1,0,2:T(8,128)(2,1)S(1)}, u32[]{:S(2)}, u32[]{:S(2)}) collective-permute-start(bf16[3,75,1,257]{3,1,0,2:T(8,128)(2,1)S(1)} %collective-permute-done.1), channel_id=1, source_target_pairs={{0,32},{32,0},{16,48},{48,16},{64,96},{96,64},{80,112},{112,80},{1... | collective-permute-start | bytes 346958 | tf_op jit(solution)/shard_map/ppermute | solution.py:29
  28.3 8.7 %collective-permute-start.3 = (bf16[3,75,1,257]{3,1,0,2:T(8,128)(2,1)S(1)}, bf16[3,75,1,257]{3,1,0,2:T(8,128)(2,1)S(1)}, u32[]{:S(2)}, u32[]{:S(2)}) collective-permute-start(bf16[3,75,1,257]{3,1,0,2:T(8,128)(2,1)S(1)} %collective-permute-done.2), channel_id=1, source_target_pairs={{0,64},{64,0},{16,80},{80,16},{32,96},{96,32},{48,112},{112,48},{1... | collective-permute-start | bytes 346958 | tf_op jit(solution)/shard_map/ppermute | solution.py:29
  28.3 20.7 %collective-permute-start.5 = (bf16[3,75,1,257]{3,1,0,2:T(8,128)(2,1)S(1)}, bf16[3,75,1,257]{3,1,0,2:T(8,128)(2,1)S(1)}, u32[]{:S(2)}, u32[]{:S(2)}) collective-permute-start(bf16[3,75,1,257]{3,1,0,2:T(8,128)(2,1)S(1)} %pad_maximum_fusion.1), channel_id=1, source_target_pairs={{1,0},{2,1},{3,2},{4,3},{5,4},{6,5},{7,6},{8,7},{9,8},{10,9},{11,1... | collective-permute-start | bytes 346958 | tf_op jit(solution)/shard_map/ppermute | solution.py:19
  36.9 11.3 %collective-permute-start.4 = (bf16[3,75,1,257]{3,1,0,2:T(8,128)(2,1)S(1)}, bf16[3,75,1,257]{3,1,0,2:T(8,128)(2,1)S(1)}, u32[]{:S(2)}, u32[]{:S(2)}) collective-permute-start(bf16[3,75,1,257]{3,1,0,2:T(8,128)(2,1)S(1)} %collective-permute-done.3), channel_id=1, source_target_pairs={{0,128},{128,0},{16,144},{144,16},{32,160},{160,32},{48,176},{176,... | collective-permute-start | bytes 346958 | tf_op jit(solution)/shard_map/ppermute | solution.py:29
  50.2 4.1 %copy-start = (bf16[3,2400,256]{2,1,0:T(8,128)(2,1)S(1)}, bf16[3,2400,256]{2,1,0:T(8,128)(2,1)}, u32[]{:S(2)}) copy-start(bf16[3,2400,256]{2,1,0:T(8,128)(2,1)} %get-tuple-element.364) | copy-start | bytes 11059204 | tf_op jit(solution)/shard_map/while
  72.8 62.5 %collective-permute-start.10 = (f32[4,48]{1,0:T(4,128)S(1)}, f32[4,48]{1,0:T(4,128)S(1)}, u32[]{:S(2)}, u32[]{:S(2)}) collective-permute-start(f32[4,48]{1,0:T(4,128)S(1)} %fusion.122), channel_id=1, source_target_pairs={{0,16},{16,0},{32,48},{48,32},{64,80},{80,64},{96,112},{112,96},{1... | collective-permute-start | bytes 2312 | tf_op jit(solution)/shard_map/ppermute | solution.py:29
  96.8 38.6 %collective-permute-start.8 = (f32[4,1,48]{2,0,1:T(4,128)S(1)}, f32[4,1,48]{2,0,1:T(4,128)S(1)}, u32[]{:S(2)}, u32[]{:S(2)}) collective-permute-start(f32[4,1,48]{2,0,1:T(4,128)S(1)} %bitcast.361), channel_id=1, source_target_pairs={{0,1},{1,2},{2,3},{3,4},{4,5},{5,6},{6,7},{7,8},{8,9},{9,10},{10,1... | collective-permute-start | bytes 2312 | tf_op jit(solution)/shard_map/ppermute | solution.py:40
  120.3 13.7 %collective-permute-start.7 = (f32[4,1,48]{2,0,1:T(4,128)S(1)}, f32[4,1,48]{2,0,1:T(4,128)S(1)}, u32[]{:S(2)}, u32[]{:S(2)}) collective-permute-start(f32[4,1,48]{2,0,1:T(4,128)S(1)} %convolution_bitcast_fusion.1), channel_id=1, source_target_pairs={{16,0},{32,16},{48,32},{64,48},{80,64},{96,80},{112,96},{128,112},... | collective-permute-start | bytes 2312 | tf_op jit(solution)/shard_map/ppermute | solution.py:42
  123.6 7.7 %collective-permute-start.6 = (f32[4,1,48]{2,0,1:T(4,128)S(1)}, f32[4,1,48]{2,0,1:T(4,128)S(1)}, u32[]{:S(2)}, u32[]{:S(2)}) collective-permute-start(f32[4,1,48]{2,0,1:T(4,128)S(1)} %convolution_bitcast_fusion.2), channel_id=1, source_target_pairs={{0,16},{16,32},{32,48},{48,64},{64,80},{80,96},{96,112},{112,128},... | collective-permute-start | bytes 2312 | tf_op jit(solution)/shard_map/ppermute | solution.py:40
  124.0 13.1 %collective-permute-start.9 = (f32[4,1,48]{2,0,1:T(4,128)S(1)}, f32[4,1,48]{2,0,1:T(4,128)S(1)}, u32[]{:S(2)}, u32[]{:S(2)}) collective-permute-start(f32[4,1,48]{2,0,1:T(4,128)S(1)} %convolution_bitcast_fusion), channel_id=1, source_target_pairs={{1,0},{2,1},{3,2},{4,3},{5,4},{6,5},{7,6},{8,7},{9,8},{10,9},{11,1... | collective-permute-start | bytes 2312 | tf_op jit(solution)/shard_map/ppermute | solution.py:42
  135.3 3.7 %collective-permute-start.11 = (f32[4,48]{1,0:T(4,128)S(1)}, f32[4,48]{1,0:T(4,128)S(1)}, u32[]{:S(2)}, u32[]{:S(2)}) collective-permute-start(f32[4,48]{1,0:T(4,128)S(1)} %collective-permute-done.10), channel_id=1, source_target_pairs={{0,32},{32,0},{16,48},{48,16},{64,96},{96,64},{80,112},{112,80},{1... | collective-permute-start | bytes 2312 | tf_op jit(solution)/shard_map/ppermute | solution.py:29
  139.0 4.5 %collective-permute-start.12 = (f32[4,48]{1,0:T(4,128)S(1)}, f32[4,48]{1,0:T(4,128)S(1)}, u32[]{:S(2)}, u32[]{:S(2)}) collective-permute-start(f32[4,48]{1,0:T(4,128)S(1)} %collective-permute-done.11), channel_id=1, source_target_pairs={{0,64},{64,0},{16,80},{80,16},{32,96},{96,32},{48,112},{112,48},{1... | collective-permute-start | bytes 2312 | tf_op jit(solution)/shard_map/ppermute | solution.py:29
  143.5 7.5 %collective-permute-start.13 = (f32[4,48]{1,0:T(4,128)S(1)}, f32[4,48]{1,0:T(4,128)S(1)}, u32[]{:S(2)}, u32[]{:S(2)}) collective-permute-start(f32[4,48]{1,0:T(4,128)S(1)} %collective-permute-done.12), channel_id=1, source_target_pairs={{0,128},{128,0},{16,144},{144,16},{32,160},{160,32},{48,176},{176,... | collective-permute-start | bytes 2312 | tf_op jit(solution)/shard_map/ppermute | solution.py:29
where the time goes:
time: 155 us
  starting transfers between devices  69 us (45%)
  waiting for transfers between devices  37.2 us (24%)
  matrix products  25.6 us (17%)
  local copies, waits for them, and re-layouts  8.93 us (6%)
  other arithmetic  6.87 us (4%)
  between operations  6.74 us (4%)
    ppermute x8, waiting for transfers between devices, swapped(): return lax.ppermute(block, axis, route)  37.2 us
    ppermute x8, starting transfers between devices, swapped(): return lax.ppermute(block, axis, route)  27.5 us
    ppermute x2, starting transfers between devices, extended(): lax.ppermute(tail, axis, [(i, (i + 1) % count) for i in range(ends)])  23.3 us
    dot_general x6, matrix products, sample(): combined = jnp.dot(w_main, planes[comp], preferred_element_type=jnp.float32)  14.8 us
    ppermute x2, starting transfers between devices, extended(): lax.ppermute(head, axis, [((i + 1) % count, i) for i in range(ends)])  9.37 us
    ppermute x1, starting transfers between devices, shifted(): return lax.ppermute(block, axis, route)  6.94 us
    dot_general x2, matrix products, sample(): east_sum = jnp.dot(w_main, east_col.T, preferred_element_type=jnp.float32)  4.28 us
    unnamed x14, local copies, waits for them, and re-layouts  3.78 us
  transfers between devices with their start and end apart: 14, of which 7 were waited for; matrix products, arithmetic and copies ran while one was open for 8% of the time, Pallas kernels for 0%

commit v1 on v0

v1 whole, which is shorter than its diff:
```python
import functools

import jax
import jax.numpy as jnp
from jax import lax
from jax.experimental import pallas as pl
from jax.experimental.pallas import tpu as pltpu
from jax.sharding import PartitionSpec as P

MESH = pl.DeviceIdType.MESH
CAP = 48
LANES = 128
F32, BF16, I32 = jnp.float32, jnp.bfloat16, jnp.int32
NT = (((1,), (1,)), ((), ()))
TN = (((0,), (0,)), ((), ()))


def iota(shape, dim):
    return lax.broadcasted_iota(I32, shape, dim)


def thirds(x):
    high = x.astype(BF16)
    rest = x - high.astype(F32)
    mid = rest.astype(BF16)
    low = (rest - mid.astype(F32)).astype(BF16)
    return jnp.concatenate([high.astype(F32), mid.astype(F32), low.astype(F32)], axis=0).astype(BF16)


def placed(records, target, size):
    onehot = jnp.where(iota((size, target.shape[1]), 0) == target, 1.0, 0.0).astype(BF16)
    out = lax.dot_general(thirds(records), onehot, NT, preferred_element_type=F32)
    return out[0:8] + out[8:16] + out[16:24]


def velocity_at(corners, a_row, b_row, c_row):
    sub = iota((8, a_row.shape[1]), 0)
    wb = jnp.where(sub < 4, 1.0 - b_row, b_row)
    w0 = (wb * (1.0 - c_row)).astype(BF16).astype(F32)
    w1 = (wb * c_row).astype(BF16).astype(F32)
    sums = []
    for d in range(2):
        s = w0 * corners[0][d] + w1 * corners[1][d]
        sums.append(s + pltpu.roll(s, 4, 0))
    return (1.0 - a_row) * sums[0] + a_row * sums[1]


def kernel(
    dims, vel_hbm, off_ref, cell_ref, cell_smem, count_smem, move_ref,
    new_off, new_cell, new_count,
    vel, table, gathered, posit, ect, nrow, nfold, cnr, cfold, ect_in, nrow_in, cnr_in,
    pack, pack_in, vsem, send, recv, lsem,
):
    depth, rows, cols, slots, live, n_lat, n_lon = dims
    wide = pl.cdiv(live, LANES) * LANES
    tiles = wide // LANES
    level = rows * 4
    span = table.shape[0] // 3
    r, p = lax.axis_index("lat"), lax.axis_index("lon")
    east, west = lax.rem(p + 1, n_lon), lax.rem(p + n_lon - 1, n_lon)
    across, corner = n_lon - 1 - p, lax.rem(n_lon - p, n_lon)
    top = r == n_lat - 1
    away = jnp.logical_and(top, corner != p)

    loads = [pltpu.make_async_copy(vel_hbm.at[c], vel.at[c], vsem.at[c]) for c in range(3)]
    for load in loads:
        load.start()

    barrier = pltpu.get_barrier_semaphore()

    def greet(lat, lon):
        pl.semaphore_signal(barrier, inc=1, device_id=(lon, lat), device_id_type=MESH)

    greet(r, east)
    greet(r, west)

    @pl.when(r < n_lat - 1)
    def _():
        greet(r + 1, p)
        greet(r + 1, east)

    @pl.when(r > 0)
    def _():
        greet(r - 1, p)

    @pl.when(top)
    def _():
        greet(r, across)

    @pl.when(away)
    def _():
        greet(r, corner)

    lane = iota((8, LANES), 1)
    lane_rows = iota((rows, LANES), 1)
    for part in range(3):
        table[pl.ds(part * span + depth * level, span - depth * level), :] = jnp.zeros(
            (span - depth * level, LANES), F32
        )
    cnr[...] = jnp.zeros_like(cnr)
    for c in range(3):
        loads[c].wait()

        def build(k, column):
            low = vel[c, k, :, 0:LANES].astype(F32)
            high = vel[c, k, :, LANES : 2 * LANES].astype(F32)
            seam = jnp.where(lane_rows == LANES - 1, low, high)
            for s in range(rows // 8):
                at = k * level + 32 * s + c
                part = slice(8 * s, 8 * s + 8)
                table[pl.ds(at, 8, stride=4), :] = low[part]
                table[pl.ds(at + span, 8, stride=4), :] = seam[part]
                table[pl.ds(at + 2 * span, 8, stride=4), :] = high[part]
            return jnp.where(lane_rows == k, pltpu.roll(low, k, 1), column)

        column = lax.fori_loop(0, depth, build, jnp.zeros((rows, LANES), F32))
        ect[c] = column.astype(BF16)
        cnr[c : c + 1, :] = column[0:1]

        @pl.when(top)
        def _(c=c, column=column):
            cfold[c : c + 1, :] = column[rows - 1 : rows]

    def edge(target, row):
        for c in range(3):
            for half in range(2):
                for block in range(nrow.shape[0] // 16):
                    at = 2 * half * span + block * 16 * level + 4 * row + c
                    pair = [table[pl.ds(at + u * 8 * level, 8, stride=level), :] for u in range(2)]
                    target[pl.ds(block * 16, 16), pl.ds(c * cols + half * LANES, LANES)] = jnp.concatenate(
                        pair, axis=0
                    ).astype(BF16)

    edge(nrow, 0)

    @pl.when(top)
    def _():
        edge(nfold, rows - 1)

    def remote(src, dst, s, t, lat, lon):
        return pltpu.make_async_remote_copy(
            src, dst, send.at[s], recv.at[t], device_id=(lon, lat), device_id_type=MESH
        )

    ect_out = remote(ect, ect_in, 0, 0, r, west)
    row_out = remote(nrow, nrow_in, 1, 1, r - 1, p)
    cnr_out = remote(cnr, cnr_in, 2, 2, r - 1, west)
    fold_out = remote(nfold, nrow_in, 3, 1, r, across)
    cfold_out = remote(cfold, cnr_in, 4, 2, r, corner)
    cfold_here = pltpu.make_async_copy(cfold, cnr_in, lsem)

    peers = 2 + 2 * (r > 0).astype(I32) + (r < n_lat - 1).astype(I32) + top.astype(I32) + away.astype(I32)
    pl.semaphore_wait(barrier, peers)

    @pl.when(r > 0)
    def _():
        row_out.start()
        cnr_out.start()

    @pl.when(top)
    def _():
        fold_out.start()

    @pl.when(away)
    def _():
        cfold_out.start()

    @pl.when(jnp.logical_and(top, corner == p))
    def _():
        cfold_here.start()

    ect_out.start()

    for block in range(tiles):
        def gather(step, accs):
            accs = list(accs)
            base = step * 8
            ahead = lane - base
            for u in range(8):
                slot = block * LANES + base + u
                i, j, k = (cell_smem[n, 0, slot] for n in range(3))
                part = jnp.where(i == LANES - 1, span, jnp.where(i >= LANES, 2 * span, 0))
                at = part + k * level + 4 * j
                shift = (base + u - i) & (LANES - 1)
                here = ahead == u
                there = (ahead == u + 1) if u < 7 else ((lane == ((base + 8) & (LANES - 1))))
                for dk in range(2):
                    turned = pltpu.roll(table[pl.ds(at + dk * level, 8), :], shift, 1)
                    accs[2 * dk] = jnp.where(here, turned, accs[2 * dk])
                    accs[2 * dk + 1] = jnp.where(there, turned, accs[2 * dk + 1])
            return tuple(accs)

        count = min(LANES, live - block * LANES)
        zero = jnp.zeros((8, LANES), F32)
        accs = lax.fori_loop(0, count // 8, gather, (zero,) * 4)
        for dk in range(2):
            gathered[dk, 0, :, pl.ds(block * LANES, LANES)] = accs[2 * dk]
            gathered[dk, 1, :, pl.ds(block * LANES, LANES)] = pltpu.roll(accs[2 * dk + 1], LANES - 1, 1)

    sub = iota((8, wide), 0)
    i_row, j_row, k_row = (cell_ref[n, :, 0:wide] for n in range(3))
    motion = move_ref[:, 0:wide]
    valid = iota((1, wide), 1) < count_smem[0, 0]
    chosen = jnp.where((sub == motion) & valid, 1.0, 0.0)
    before = jnp.where(iota((LANES, LANES), 0) < iota((LANES, LANES), 1), 1.0, 0.0).astype(BF16)
    upto = jnp.concatenate([before, jnp.ones((LANES, LANES), BF16)], axis=1)
    total = jnp.zeros((8, LANES), F32)
    ranks = []
    for t in range(tiles):
        sums = jnp.dot(
            chosen[:, t * LANES : (t + 1) * LANES].astype(BF16), upto, preferred_element_type=F32
        )
        ranks.append(sums[:, :LANES] + total)
        total = total + sums[:, LANES:]
    rank = jnp.concatenate(ranks, axis=1)
    stay_to = jnp.where(chosen[0:1] > 0.5, rank[0:1], -1.0).astype(I32)
    slot_to = rank + (LANES * (sub - 1)).astype(F32)
    leaving = (sub >= 1) & (chosen > 0.5)
    leave_to = (jnp.sum(jnp.where(leaving, slot_to + 1.0, 0.0), axis=0, keepdims=True) - 1.0).astype(I32)
    folding = (motion == 3) & top
    last_i, last_j = cols - 1, rows - 1
    new_i = jnp.where(
        motion == 1, 0, jnp.where(motion == 2, last_i, jnp.where(folding, last_i - i_row, i_row))
    )
    new_j = jnp.where(
        motion == 3, jnp.where(top, last_j, 0), jnp.where(motion == 4, last_j, j_row)
    )
    code = (1 + new_i + cols * (new_j + rows * k_row)).astype(F32)

    at_level = [
        jnp.where(iota((LANES, wide), 0) == k_row + dk, 1.0, 0.0).astype(BF16) for dk in range(2)
    ]
    first_col = jnp.where(top, cols - i_row, i_row)
    second_col = jnp.where(top, cols - 1 - i_row, i_row + 1)
    sign = jnp.where(top, -1.0, 1.0)

    ect_out.wait_recv()
    eastern = [[None, None], [None, None]]
    for dk in range(2):
        found = lax.dot_general(
            ect_in[...].reshape(3 * rows, LANES), at_level[dk], (((1,), (0,)), ((), ())),
            preferred_element_type=F32,
        )
        row_id = iota((rows, wide), 0)
        out = jnp.zeros((8, wide), F32)
        for dj in range(2):
            for c in range(3):
                value = jnp.sum(
                    jnp.where(row_id == j_row + dj, found[c * rows : (c + 1) * rows], 0.0), axis=0, keepdims=True
                )
                out = jnp.where(sub == 4 * dj + c, value, out)
        eastern[dk] = out

    row_out.wait_recv()
    cnr_wait = remote(cnr, cnr_in, 2, 2, r, west)

    @pl.when(jnp.logical_or(jnp.logical_not(top), corner != p))
    def _():
        cnr_wait.wait_recv()

    @pl.when(jnp.logical_and(top, corner == p))
    def _():
        cfold_here.wait()

    northern = [[], []]
    corner_at = [
        jnp.dot(cnr_in[...].astype(BF16), at_level[dk], preferred_element_type=F32) for dk in range(2)
    ]
    col_id = iota((cols, LANES), 0)
    for t in range(tiles):
        part = slice(t * LANES, (t + 1) * LANES)
        hits = [col_id == first_col[:, part], col_id == second_col[:, part]]
        for dk in range(2):
            outs = [jnp.zeros((8, LANES), F32), jnp.zeros((8, LANES), F32)]
            for c in range(3):
                found = lax.dot_general(
                    nrow_in[:, c * cols : (c + 1) * cols], at_level[dk][0 : nrow_in.shape[0], part], TN,
                    preferred_element_type=F32,
                )
                for d in range(2):
                    value = jnp.sum(jnp.where(hits[d], found, 0.0), axis=0, keepdims=True)
                    outs[d] = jnp.where(iota((8, LANES), 0) == 4 + c, value, outs[d])
            northern[dk].append(outs)

    corners = [[None, None], [None, None]]
    lower = sub >= 4
    for dk in range(2):
        edge_value = pltpu.roll(corner_at[dk], 4, 0)
        for d in range(2):
            at_col = first_col if d == 0 else second_col
            north = jnp.concatenate([northern[dk][t][d] for t in range(tiles)], axis=1)
            north = sign * jnp.where(at_col == cols, edge_value, north)
            here = gathered[dk, d]
            if d == 1:
                here = jnp.where(i_row == cols - 1, eastern[dk], here)
            corners[dk][d] = jnp.where(lower & (j_row == rows - 1), north, here)

    posit[...] = jnp.zeros_like(posit)
    for n in range(3):
        posit[n : n + 1, :] = off_ref[n, :, 0:wide]
    position = posit[...]
    first = velocity_at(corners, position[0:1], position[1:2], position[2:3])
    middle = position + 0.5 * first
    moved = position + velocity_at(corners, middle[0:1], middle[1:2], middle[2:3])
    na, nb, nc = moved[0:1], moved[1:2], moved[2:3]
    new_a = jnp.where(
        motion == 1, na - 1.0, jnp.where(motion == 2, na + 1.0, jnp.where(folding, 1.0 - na, na))
    )
    new_b = jnp.where(
        motion == 3, jnp.where(top, 2.0 - nb, nb - 1.0), jnp.where(motion == 4, nb + 1.0, nb)
    )
    records = jnp.where(
        sub == 0, new_a, jnp.where(sub == 1, new_b, jnp.where(sub == 2, nc, jnp.where(sub == 3, code, 0.0)))
    )

    packets = placed(records, leave_to, 4 * LANES)
    for m in range(4):
        pack[m] = packets[:, m * LANES : (m + 1) * LANES]

    @pl.when(r == 0)
    def _():
        pack_in[2] = jnp.zeros((8, LANES), F32)

    east_out = remote(pack.at[0], pack_in.at[0], 5, 3, r, east)
    west_out = remote(pack.at[1], pack_in.at[1], 6, 4, r, west)
    north_out = remote(pack.at[2], pack_in.at[2], 7, 5, r + 1, p)
    over_out = remote(pack.at[2], pack_in.at[3], 7, 6, r, across)
    south_out = remote(pack.at[3], pack_in.at[3], 8, 6, r - 1, p)

    @pl.when(top)
    def _():
        over_out.start()

    @pl.when(r < n_lat - 1)
    def _():
        north_out.start()

    @pl.when(r > 0)
    def _():
        south_out.start()

    east_out.start()
    west_out.start()

    kept = placed(records, stay_to, wide)
    filled = total[0:1, :]

    east_out.wait_recv()
    west_out.wait_recv()

    @pl.when(r > 0)
    def _():
        north_out.wait_recv()

    over_out.wait_recv()

    arrivals = jnp.concatenate([pack_in[m] for m in range(4)], axis=1)
    lanes_row = iota((1, LANES), 1).astype(F32)
    targets = []
    for m in range(4):
        present = jnp.where(arrivals[3:4, m * LANES : (m + 1) * LANES] > 0.5, 1.0, 0.0)
        targets.append(jnp.where(present > 0.5, filled + lanes_row, -1.0))
        filled = filled + jnp.sum(present, axis=1, keepdims=True)
    joined = placed(arrivals, jnp.concatenate(targets, axis=1).astype(I32), slots)
    result = joined + jnp.concatenate([kept, jnp.zeros((8, slots - wide), F32)], axis=1)
    decoded = jnp.maximum(result[3:4].astype(I32) - 1, 0)
    for n in range(3):
        new_off[n] = result[n : n + 1]
    new_cell[0] = decoded & (cols - 1)
    new_cell[1] = (decoded // cols) & (rows - 1)
    new_cell[2] = decoded // (cols * rows)
    new_count[...] = filled[:, 0:1].astype(I32)

    ect_out.wait_send()
    east_out.wait_send()
    west_out.wait_send()
    north_out.wait_send()

    @pl.when(r > 0)
    def _():
        row_out.wait_send()
        cnr_out.wait_send()
        south_out.wait_send()

    @pl.when(top)
    def _():
        fold_out.wait_send()

    @pl.when(away)
    def _():
        cfold_out.wait_send()


def shards(velocity, offsets, cells, counts, moves):
    _, depth, rows, cols = velocity.shape
    slots = offsets.shape[2]
    live = slots * 3 // 4
    wide = pl.cdiv(live, LANES) * LANES
    deep = pl.cdiv(depth, 16) * 16
    dims = (depth, rows, cols, slots, live, lax.axis_size("lat"), lax.axis_size("lon"))
    vmem = pl.BlockSpec(memory_space=pltpu.VMEM)
    smem = pl.BlockSpec(memory_space=pltpu.SMEM)
    return pl.pallas_call(
        functools.partial(kernel, dims),
        out_shape=(
            jax.ShapeDtypeStruct((3, 1, slots), F32),
            jax.ShapeDtypeStruct((3, 1, slots), I32),
            jax.ShapeDtypeStruct((1, 1), I32),
        ),
        in_specs=[pl.BlockSpec(memory_space=pl.ANY), vmem, vmem, smem, smem, vmem],
        out_specs=(vmem, vmem, vmem),
        scratch_shapes=[
            pltpu.VMEM((3, depth, rows, cols), BF16),
            pltpu.VMEM((3 * deep * rows * 4, LANES), F32),
            pltpu.VMEM((2, 2, 8, wide), F32),
            pltpu.VMEM((8, wide), F32),
            pltpu.VMEM((3, rows, LANES), BF16),
            pltpu.VMEM((deep, 3 * cols), BF16),
            pltpu.VMEM((deep, 3 * cols), BF16),
            pltpu.VMEM((8, LANES), F32),
            pltpu.VMEM((8, LANES), F32),
            pltpu.VMEM((3, rows, LANES), BF16),
            pltpu.VMEM((deep, 3 * cols), BF16),
            pltpu.VMEM((8, LANES), F32),
            pltpu.VMEM((4, 8, LANES), F32),
            pltpu.VMEM((4, 8, LANES), F32),
            pltpu.SemaphoreType.DMA((3,)),
            pltpu.SemaphoreType.DMA((9,)),
            pltpu.SemaphoreType.DMA((7,)),
            pltpu.SemaphoreType.DMA,
        ],
        compiler_params=pltpu.CompilerParams(
            collective_id=0, has_side_effects=True, vmem_limit_bytes=48 * 1024 * 1024
        ),
        name="advance",
    )(velocity, offsets, cells, cells, counts, moves)


def solution(mesh):
    placed_in = (
        P(None, None, "lat", "lon"),
        P(None, "lat", "lon"),
        P(None, "lat", "lon"),
        P("lat", "lon"),
        P("lat", "lon"),
    )
    return jax.shard_map(
        shards,
        mesh=mesh,
        in_specs=placed_in,
        out_specs=(P(None, "lat", "lon"), P(None, "lat", "lon"), P("lat", "lon")),
        check_vma=False,
    )
```

time: 155 us -> 47.2 us (0.30)
  the two profiles are of different devices: /device:TPU:4 before, /device:TPU:1 now
where the time goes in v1:
time: 47.2 us; the launch traced here: 46.9 us
  Pallas kernels  38.6 us (82%)
  local copies, waits for them, and re-layouts  5.32 us (11%)
  between operations  3.05 us (6%)
    pallas_call x1, Pallas kernels, shards(): pl.pallas_call(functools.partial(kernel, dims), out_shape=(jax.ShapeDtype...  38.6 us
    unnamed x10, local copies, waits for them, and re-layouts  5.32 us

profile of v1, /device:TPU:1, one launch (start us, length us, event | category | flops | bytes accessed | tf_op | source)
XLA Modules:
  0.0 46.9 jit_solution(14789269587458906403)
XLA Ops:
  1.3 0.0 copy-start
  1.3 2.0 %copy-done = bf16[3,75,32,256]{3,2,1,0:T(8,128)(2,1)S(1)} copy-done((bf16[3,75,32,256]{3,2,1,0:T(8,128)(2,1)S(1)}, bf16[3,75,32,256]{3,2,1,0:T(8,128)(2,1)}, u32[]{:S(2)}) %copy-start) | copy-done | bytes 3686424
  3.3 0.0 copy-start.1
  3.3 0.7 %copy-done.1 = s32[3,1,768]{2,1,0:T(1,128)S(1)} copy-done((s32[3,1,768]{2,1,0:T(1,128)S(1)}, s32[3,1,768]{2,1,0:T(1,128)}, u32[]{:S(2)}) %copy-start.1) | copy-done | bytes 9240
  4.0 0.0 copy-start.2
  4.0 0.7 %copy-done.2 = f32[3,1,768]{2,1,0:T(1,128)S(1)} copy-done((f32[3,1,768]{2,1,0:T(1,128)S(1)}, f32[3,1,768]{2,1,0:T(1,128)}, u32[]{:S(2)}) %copy-start.2) | copy-done | bytes 9240
  4.7 0.0 copy-start.3
  4.7 0.7 %copy-done.3 = s32[1,768]{1,0:T(1,128)S(1)} copy-done((s32[1,768]{1,0:T(1,128)S(1)}, s32[1,768]{1,0:T(1,128)}, u32[]{:S(2)}) %copy-start.3) | copy-done | bytes 3096
  5.4 38.6 %advance.1 = (f32[3,1,768]{2,1,0:T(1,128)S(1)}, s32[3,1,768]{2,1,0:T(1,128)S(1)}, s32[1,1]{1,0:T(1,128)}) custom-call(bf16[3,75,32,256]{3,2,1,0:T(8,128)(2,1)S(1)} %copy-done, f32[3,1,768]{2,1,0:T(1,128)S(1)} %copy-done.2, s32[3,1,768]{2,1,0:T(1,128)S(1)} %copy-done.1, s32[3,1,768]{2,1,0:T(1,128)S(1)} %copy-done.1, s32[1,1]{1,0:T(1,128)S(6)} %copy.11.count_smem, ...), custom_call_target="tpu_custom_call" | custom-call | tf_op jit(solution)/shard_map/advance/pallas_call | solution.py:403
  44.0 0.6 %copy.12 = f32[3,1,768]{2,1,0:T(1,128)} copy(f32[3,1,768]{2,1,0:T(1,128)S(1)} %get-tuple-element.6) | data formatting | bytes 18432
  44.6 0.6 %copy.13 = s32[3,1,768]{2,1,0:T(1,128)} copy(s32[3,1,768]{2,1,0:T(1,128)S(1)} %get-tuple-element.7) | data formatting | bytes 18432
Async XLA Ops:
  1.3 2.0 %copy-start = (bf16[3,75,32,256]{3,2,1,0:T(8,128)(2,1)S(1)}, bf16[3,75,32,256]{3,2,1,0:T(8,128)(2,1)}, u32[]{:S(2)}) copy-start(bf16[3,75,32,256]{3,2,1,0:T(8,128)(2,1)} %vel_hbm.1) | copy-start | bytes 11059204
  3.3 0.7 %copy-start.1 = (s32[3,1,768]{2,1,0:T(1,128)S(1)}, s32[3,1,768]{2,1,0:T(1,128)}, u32[]{:S(2)}) copy-start(s32[3,1,768]{2,1,0:T(1,128)} %cell_smem.1) | copy-start | bytes 27652
  4.0 0.7 %copy-start.2 = (f32[3,1,768]{2,1,0:T(1,128)S(1)}, f32[3,1,768]{2,1,0:T(1,128)}, u32[]{:S(2)}) copy-start(f32[3,1,768]{2,1,0:T(1,128)} %off_ref.1) | copy-start | bytes 27652
  4.7 0.7 %copy-start.3 = (s32[1,768]{1,0:T(1,128)S(1)}, s32[1,768]{1,0:T(1,128)}, u32[]{:S(2)}) copy-start(s32[1,768]{1,0:T(1,128)} %move_ref.1) | copy-start | bytes 9220

commit v2 on v1

v2 whole, which is shorter than its diff:
```python
import functools

import jax
import jax.numpy as jnp
from jax import lax
from jax.experimental import pallas as pl
from jax.experimental.pallas import tpu as pltpu
from jax.sharding import PartitionSpec as P

MESH = pl.DeviceIdType.MESH
CAP = 48
LANES = 128
F32, BF16, I32 = jnp.float32, jnp.bfloat16, jnp.int32
NT = (((1,), (1,)), ((), ()))
TN = (((0,), (0,)), ((), ()))


def iota(shape, dim):
    return lax.broadcasted_iota(I32, shape, dim)


def thirds(x):
    high = x.astype(BF16)
    rest = x - high.astype(F32)
    mid = rest.astype(BF16)
    low = (rest - mid.astype(F32)).astype(BF16)
    return jnp.concatenate([high.astype(F32), mid.astype(F32), low.astype(F32)], axis=0).astype(BF16)


def slots_of(target, size):
    return jnp.where(iota((size, target.shape[1]), 0) == target, 1.0, 0.0).astype(BF16)


def placed(records, onehot):
    out = lax.dot_general(thirds(records), onehot, NT, preferred_element_type=F32)
    return out[0:8] + out[8:16] + out[16:24]


def velocity_at(corners, a_row, b_row, c_row):
    sub = iota((8, a_row.shape[1]), 0)
    wb = jnp.where(sub < 4, 1.0 - b_row, b_row)
    w0 = (wb * (1.0 - c_row)).astype(BF16).astype(F32)
    w1 = (wb * c_row).astype(BF16).astype(F32)
    sums = []
    for d in range(2):
        s = w0 * corners[0][d] + w1 * corners[1][d]
        sums.append(s + pltpu.roll(s, 4, 0))
    return (1.0 - a_row) * sums[0] + a_row * sums[1]


def kernel(
    dims, vel_hbm, off_hbm, cell_hbm, count_smem, move_hbm,
    new_off, new_cell, new_count,
    vel, off_ref, cell_ref, move_ref, table, where_ref, where_smem, gathered, posit, stay_ref, leave_ref,
    side, column, nrow, nfold, col_in, nrow_in, cnr_in,
    pack, pack_in, vsem, isem, send, recv, lsem, asem,
):
    depth, rows, cols, slots, live, n_lat, n_lon = dims
    wide = pl.cdiv(live, LANES) * LANES
    tiles = wide // LANES
    level = rows * 4
    span = table.shape[0] // 2
    per = LANES // rows
    groups = side.shape[1]
    r, p = lax.axis_index("lat"), lax.axis_index("lon")
    east, west = lax.rem(p + 1, n_lon), lax.rem(p + n_lon - 1, n_lon)
    across, corner = n_lon - 1 - p, lax.rem(n_lon - p, n_lon)
    top = r == n_lat - 1
    away = jnp.logical_and(top, corner != p)

    smalls = [(cell_hbm, cell_ref), (move_hbm, move_ref), (off_hbm, off_ref)]
    smalls = [pltpu.make_async_copy(src, dst, isem.at[n]) for n, (src, dst) in enumerate(smalls)]
    smalls[0].start()
    loads = [pltpu.make_async_copy(vel_hbm.at[c], vel.at[c], vsem.at[c]) for c in range(3)]
    for load in loads:
        load.start()
    for small in smalls[1:]:
        small.start()

    barrier = pltpu.get_barrier_semaphore()

    def greet(lat, lon):
        pl.semaphore_signal(barrier, inc=1, device_id=(lon, lat), device_id_type=MESH)

    greet(r, east)
    greet(r, west)

    @pl.when(r < n_lat - 1)
    def _():
        greet(r + 1, p)
        greet(r + 1, east)

    @pl.when(r > 0)
    def _():
        greet(r - 1, p)

    @pl.when(top)
    def _():
        greet(r, across)

    @pl.when(away)
    def _():
        greet(r, corner)

    lane = iota((8, LANES), 1)
    sub = iota((8, wide), 0)
    smalls[0].wait()
    i_row, j_row, k_row = (cell_ref[n, :, 0:wide] for n in range(3))
    start = jnp.where(i_row >= LANES, span, 0) + k_row * level + 4 * j_row
    start = start * LANES + ((iota((1, wide), 1) - i_row) & (LANES - 1))
    for t in range(tiles):
        part = start[:, t * LANES : (t + 1) * LANES]
        where_ref[2 * t : 2 * t + 1, :] = part
        where_ref[2 * t + 1 : 2 * t + 2, :] = pltpu.roll(part, LANES // 2, 1)
    addresses = pltpu.make_async_copy(where_ref, where_smem, asem)
    addresses.start()

    for part in range(2):
        table[pl.ds(part * span + depth * level, span - depth * level), :] = jnp.zeros(
            (span - depth * level, LANES), F32
        )
    side[...] = jnp.zeros_like(side)
    first_lane = jnp.where(lane == 0, 1.0, 0.0).astype(BF16)
    for c in range(3):
        loads[c].wait()

        def build(step, carry):
            for u in range(5):
                k = step * 5 + u
                for half in range(2):
                    plane = vel[c, k, :, half * LANES : (half + 1) * LANES].astype(F32)
                    for s in range(rows // 8):
                        at = half * span + k * level + 32 * s + c
                        table[pl.ds(at, 8, stride=4), :] = plane[8 * s : 8 * s + 8]
            return carry

        lax.fori_loop(0, depth // 5, build, 0)

        for half in range(2):
            plane = vel[c, :, :, half * LANES : (half + 1) * LANES].reshape(depth * rows, LANES)
            line = lax.dot_general(first_lane, plane, NT, preferred_element_type=F32)[0:1]
            for g in range(pl.cdiv(depth, per)):
                n = min(LANES, depth * rows - g * LANES)
                side[half * 3 + c, g : g + 1, 0:n] = line[:, g * LANES : g * LANES + n]
    column[...] = side[0:3].astype(BF16)

    def edge(target, row):
        for c in range(3):
            for half in range(2):
                for block in range(nrow.shape[0] // 16):
                    at = half * span + block * 16 * level + 4 * row + c
                    pair = [table[pl.ds(at + u * 8 * level, 8, stride=level), :] for u in range(2)]
                    target[pl.ds(block * 16, 16), pl.ds(c * cols + half * LANES, LANES)] = jnp.concatenate(
                        pair, axis=0
                    ).astype(BF16)

    edge(nrow, 0)

    @pl.when(top)
    def _():
        edge(nfold, rows - 1)

    def remote(src, dst, s, t, lat, lon):
        return pltpu.make_async_remote_copy(
            src, dst, send.at[s], recv.at[t], device_id=(lon, lat), device_id_type=MESH
        )

    col_out = remote(column, col_in, 0, 0, r, west)
    row_out = remote(nrow, nrow_in, 1, 1, r - 1, p)
    cnr_out = remote(column, cnr_in, 2, 2, r - 1, west)
    fold_out = remote(nfold, nrow_in, 3, 1, r, across)
    cfold_out = remote(column, cnr_in, 4, 2, r, corner)
    cfold_here = pltpu.make_async_copy(column, cnr_in, lsem)

    peers = 2 + 2 * (r > 0).astype(I32) + (r < n_lat - 1).astype(I32) + top.astype(I32) + away.astype(I32)
    pl.semaphore_wait(barrier, peers)

    @pl.when(r > 0)
    def _():
        row_out.start()
        cnr_out.start()

    @pl.when(top)
    def _():
        fold_out.start()

    @pl.when(away)
    def _():
        cfold_out.start()

    @pl.when(jnp.logical_and(top, corner == p))
    def _():
        cfold_here.start()

    col_out.start()

    gathered[...] = jnp.zeros_like(gathered)
    for small in smalls[1:]:
        small.wait()
    addresses.wait()
    half = LANES // 2

    def gather(step, carry):
        base = (step & 1) * half
        group = step // 2
        ahead = lane - base
        accs = [gathered[n, group] for n in range(4)]
        for u in range(half):
            word = where_smem[step, u]
            at, shift = word // LANES, word & (LANES - 1)
            here = ahead == u
            there = ahead == u + 1 if u < half - 1 else lane == ((base + half) & (LANES - 1))
            for dk in range(2):
                turned = pltpu.roll(table[pl.ds(at + dk * level, 8), :], shift, 1)
                accs[2 * dk] = jnp.where(here, turned, accs[2 * dk])
                accs[2 * dk + 1] = jnp.where(there, turned, accs[2 * dk + 1])
        for n in range(4):
            gathered[n, group] = accs[n]
        return carry

    lax.fori_loop(0, live // half, gather, 0)

    motion = move_ref[:, 0:wide]
    valid = iota((1, wide), 1) < count_smem[0, 0]
    chosen = jnp.where((sub == motion) & valid, 1.0, 0.0)
    before = jnp.where(iota((LANES, LANES), 0) < iota((LANES, LANES), 1), 1.0, 0.0).astype(BF16)
    upto = jnp.concatenate([before, jnp.ones((LANES, LANES), BF16)], axis=1)
    total = jnp.zeros((8, LANES), F32)
    ranks = []
    for t in range(tiles):
        sums = jnp.dot(
            chosen[:, t * LANES : (t + 1) * LANES].astype(BF16), upto, preferred_element_type=F32
        )
        ranks.append(sums[:, :LANES] + total)
        total = total + sums[:, LANES:]
    rank = jnp.concatenate(ranks, axis=1)
    stay_to = jnp.where(chosen[0:1] > 0.5, rank[0:1], -1.0).astype(I32)
    slot_to = rank + (LANES * (sub - 1)).astype(F32)
    leaving = (sub >= 1) & (chosen > 0.5)
    leave_to = (jnp.sum(jnp.where(leaving, slot_to + 1.0, 0.0), axis=0, keepdims=True) - 1.0).astype(I32)
    stay_ref[...] = slots_of(stay_to, wide)
    leave_ref[...] = slots_of(leave_to, 4 * LANES)
    folding = (motion == 3) & top
    last_i, last_j = cols - 1, rows - 1
    new_i = jnp.where(
        motion == 1, 0, jnp.where(motion == 2, last_i, jnp.where(folding, last_i - i_row, i_row))
    )
    new_j = jnp.where(
        motion == 3, jnp.where(top, last_j, 0), jnp.where(motion == 4, last_j, j_row)
    )
    code = (1 + new_i + cols * (new_j + rows * k_row)).astype(F32)
    posit[...] = jnp.zeros_like(posit)
    for n in range(3):
        posit[n : n + 1, :] = off_ref[n, :, 0:wide]

    deep = nrow_in.shape[0]
    both_k = jnp.concatenate([k_row, k_row + 1], axis=1)
    at_level = jnp.where(iota((deep, 2 * wide), 0) == both_k, 1.0, 0.0).astype(BF16)
    at_group = jnp.where(iota((groups, 2 * wide), 0) == both_k // per, 1.0, 0.0).astype(BF16)
    outer = jnp.concatenate([jnp.where(i_row == cols - 1, groups, 0)] * 2, axis=1)
    at_side = jnp.where(iota((2 * groups, 2 * wide), 0) == both_k // per + outer, 1.0, 0.0).astype(BF16)
    place = (both_k & (per - 1)) * rows + jnp.concatenate([j_row] * 2, axis=1)
    first_col = jnp.where(top, cols - i_row, i_row)
    second_col = jnp.where(top, cols - 1 - i_row, i_row + 1)
    sign = jnp.where(top, -1.0, 1.0)
    sub2 = iota((8, 2 * wide), 0)
    cnr_wait = remote(column, cnr_in, 2, 2, r, west)

    col_out.wait_recv()
    row_out.wait_recv()

    @pl.when(jnp.logical_or(jnp.logical_not(top), corner != p))
    def _():
        cnr_wait.wait_recv()

    @pl.when(jnp.logical_and(top, corner == p))
    def _():
        cfold_here.wait()

    eastern = jnp.zeros((8, 2 * wide), F32)
    lane_id = iota((LANES, 2 * wide), 0)
    hits = [lane_id == place + dj for dj in range(2)]
    for c in range(3):
        lines = jnp.concatenate([side[3 + c], col_in[c].astype(F32)], axis=0).astype(BF16)
        found = lax.dot_general(lines, at_side, TN, preferred_element_type=F32)
        for dj in range(2):
            value = jnp.sum(jnp.where(hits[dj], found, 0.0), axis=0, keepdims=True)
            eastern = jnp.where(sub2 == 4 * dj + c, value, eastern)

    edge_value = jnp.zeros((8, 2 * wide), F32)
    edge_lane = rows * iota((8, LANES), 0) + jnp.where(top, rows - 1, 0)
    pick = jnp.where(lane == edge_lane, 1.0, 0.0).astype(BF16)
    for c in range(3):
        few = lax.dot_general(pick, cnr_in[c], NT, preferred_element_type=F32).astype(BF16)
        found = jnp.dot(few, at_group, preferred_element_type=F32)
        value = jnp.sum(jnp.where(sub2 == (both_k & (per - 1)), found, 0.0), axis=0, keepdims=True)
        edge_value = jnp.where(sub2 == 4 + c, value, edge_value)

    northern = [jnp.zeros((8, 2 * wide), F32) for _ in range(2)]
    col_id = iota((cols, wide), 0)
    hits = [col_id == first_col, col_id == second_col]
    for c in range(3):
        found = lax.dot_general(
            nrow_in[:, c * cols : (c + 1) * cols], at_level, TN, preferred_element_type=F32
        )
        for d in range(2):
            value = jnp.concatenate(
                [
                    jnp.sum(
                        jnp.where(hits[d], found[:, dk * wide : (dk + 1) * wide], 0.0), axis=0, keepdims=True
                    )
                    for dk in range(2)
                ],
                axis=1,
            )
            northern[d] = jnp.where(sub2 == 4 + c, value, northern[d])

    corners = [[None, None], [None, None]]
    lower = sub >= 4
    for dk in range(2):
        part = slice(dk * wide, (dk + 1) * wide)
        for d in range(2):
            at_col = first_col if d == 0 else second_col
            north = sign * jnp.where(at_col == cols, edge_value[:, part], northern[d][:, part])
            inside = [gathered[2 * dk + d, t] for t in range(tiles)]
            if d == 1:
                inside = [pltpu.roll(x, LANES - 1, 1) for x in inside]
            inside = jnp.concatenate(inside, axis=1)
            if d == 1:
                inside = jnp.where((i_row & (LANES - 1)) == LANES - 1, eastern[:, part], inside)
            corners[dk][d] = jnp.where(lower & (j_row == rows - 1), north, inside)

    position = posit[...]
    first = velocity_at(corners, position[0:1], position[1:2], position[2:3])
    middle = position + 0.5 * first
    moved = position + velocity_at(corners, middle[0:1], middle[1:2], middle[2:3])
    na, nb, nc = moved[0:1], moved[1:2], moved[2:3]
    new_a = jnp.where(
        motion == 1, na - 1.0, jnp.where(motion == 2, na + 1.0, jnp.where(folding, 1.0 - na, na))
    )
    new_b = jnp.where(
        motion == 3, jnp.where(top, 2.0 - nb, nb - 1.0), jnp.where(motion == 4, nb + 1.0, nb)
    )
    records = jnp.where(
        sub == 0, new_a, jnp.where(sub == 1, new_b, jnp.where(sub == 2, nc, jnp.where(sub == 3, code, 0.0)))
    )

    packets = placed(records, leave_ref[...])
    for m in range(4):
        pack[m] = packets[:, m * LANES : (m + 1) * LANES]

    @pl.when(r == 0)
    def _():
        pack_in[2] = jnp.zeros((8, LANES), F32)

    east_out = remote(pack.at[0], pack_in.at[0], 5, 3, r, east)
    west_out = remote(pack.at[1], pack_in.at[1], 6, 4, r, west)
    north_out = remote(pack.at[2], pack_in.at[2], 7, 5, r + 1, p)
    over_out = remote(pack.at[2], pack_in.at[3], 7, 6, r, across)
    south_out = remote(pack.at[3], pack_in.at[3], 8, 6, r - 1, p)

    @pl.when(top)
    def _():
        over_out.start()

    @pl.when(r < n_lat - 1)
    def _():
        north_out.start()

    @pl.when(r > 0)
    def _():
        south_out.start()

    east_out.start()
    west_out.start()

    kept = placed(records, stay_ref[...])
    filled = total[0:1, :]

    east_out.wait_recv()
    west_out.wait_recv()

    @pl.when(r > 0)
    def _():
        north_out.wait_recv()

    over_out.wait_recv()

    arrivals = jnp.concatenate([pack_in[m] for m in range(4)], axis=1)
    lanes_row = iota((1, LANES), 1).astype(F32)
    targets = []
    for m in range(4):
        present = jnp.where(arrivals[3:4, m * LANES : (m + 1) * LANES] > 0.5, 1.0, 0.0)
        targets.append(jnp.where(present > 0.5, filled + lanes_row, -1.0))
        filled = filled + jnp.sum(present, axis=1, keepdims=True)
    joined = placed(arrivals, slots_of(jnp.concatenate(targets, axis=1).astype(I32), slots))
    result = joined + jnp.concatenate([kept, jnp.zeros((8, slots - wide), F32)], axis=1)
    decoded = jnp.maximum(result[3:4].astype(I32) - 1, 0)
    for n in range(3):
        new_off[n] = result[n : n + 1]
    new_cell[0] = decoded & (cols - 1)
    new_cell[1] = (decoded // cols) & (rows - 1)
    new_cell[2] = decoded // (cols * rows)
    new_count[...] = filled[:, 0:1].astype(I32)

    col_out.wait_send()
    east_out.wait_send()
    west_out.wait_send()
    north_out.wait_send()

    @pl.when(r > 0)
    def _():
        row_out.wait_send()
        cnr_out.wait_send()
        south_out.wait_send()

    @pl.when(top)
    def _():
        fold_out.wait_send()

    @pl.when(away)
    def _():
        cfold_out.wait_send()


def shards(velocity, offsets, cells, counts, moves):
    _, depth, rows, cols = velocity.shape
    slots = offsets.shape[2]
    live = slots * 3 // 4
    wide = pl.cdiv(live, LANES) * LANES
    deep = pl.cdiv(depth, 16) * 16
    dims = (depth, rows, cols, slots, live, lax.axis_size("lat"), lax.axis_size("lon"))
    groups = pl.cdiv(depth * rows, 8 * LANES) * 8
    vmem = pl.BlockSpec(memory_space=pltpu.VMEM)
    hbm = pl.BlockSpec(memory_space=pl.ANY)
    return pl.pallas_call(
        functools.partial(kernel, dims),
        out_shape=(
            jax.ShapeDtypeStruct((3, 1, slots), F32),
            jax.ShapeDtypeStruct((3, 1, slots), I32),
            jax.ShapeDtypeStruct((1, 1), I32),
        ),
        in_specs=[hbm, hbm, hbm, pl.BlockSpec(memory_space=pltpu.SMEM), hbm],
        out_specs=(vmem, vmem, vmem),
        scratch_shapes=[
            pltpu.VMEM((3, depth, rows, cols), BF16),
            pltpu.VMEM((3, 1, slots), F32),
            pltpu.VMEM((3, 1, slots), I32),
            pltpu.VMEM((1, slots), I32),
            pltpu.VMEM((2 * deep * rows * 4, LANES), F32),
            pltpu.VMEM((2 * wide // LANES, LANES), I32),
            pltpu.SMEM((2 * wide // LANES, LANES), I32),
            pltpu.VMEM((4, wide // LANES, 8, LANES), F32),
            pltpu.VMEM((8, wide), F32),
            pltpu.VMEM((wide, wide), BF16),
            pltpu.VMEM((4 * LANES, wide), BF16),
            pltpu.VMEM((6, groups, LANES), F32),
            pltpu.VMEM((3, groups, LANES), BF16),
            pltpu.VMEM((deep, 3 * cols), BF16),
            pltpu.VMEM((deep, 3 * cols), BF16),
            pltpu.VMEM((3, groups, LANES), BF16),
            pltpu.VMEM((deep, 3 * cols), BF16),
            pltpu.VMEM((3, groups, LANES), BF16),
            pltpu.VMEM((4, 8, LANES), F32),
            pltpu.VMEM((4, 8, LANES), F32),
            pltpu.SemaphoreType.DMA((3,)),
            pltpu.SemaphoreType.DMA((3,)),
            pltpu.SemaphoreType.DMA((9,)),
            pltpu.SemaphoreType.DMA((7,)),
            pltpu.SemaphoreType.DMA,
            pltpu.SemaphoreType.DMA,
        ],
        compiler_params=pltpu.CompilerParams(
            collective_id=0, has_side_effects=True, vmem_limit_bytes=67043328
        ),
        name="advance",
    )(velocity, offsets, cells, counts, moves)


def solution(mesh):
    placed_in = (
        P(None, None, "lat", "lon"),
        P(None, "lat", "lon"),
        P(None, "lat", "lon"),
        P("lat", "lon"),
        P("lat", "lon"),
    )
    return jax.shard_map(
        shards,
        mesh=mesh,
        in_specs=placed_in,
        out_specs=(P(None, "lat", "lon"), P(None, "lat", "lon"), P("lat", "lon")),
        check_vma=False,
    )
```

time: 47.2 us -> 27.2 us (0.58)
  Pallas kernels: 38.6 us -> 21.3 us
  local copies, waits for them, and re-layouts: 5.32 us -> 2.6 us
    pallas_call x1, Pallas kernels: 38.6 us -> 21.3 us  [shards(): pl.pallas_call(functools.partial(kernel, dims), out_shape=(jax.ShapeDtype...]
    unnamed x10 -> x2, local copies, waits for them, and re-layouts: 5.32 us -> 2.6 us
where the time goes in v2:
time: 27.2 us; the launch traced here: 26.9 us
  Pallas kernels  21.3 us (78%)
  between operations  3.05 us (11%)
  local copies, waits for them, and re-layouts  2.6 us (10%)
    pallas_call x1, Pallas kernels, shards(): pl.pallas_call(functools.partial(kernel, dims), out_shape=(jax.ShapeDtype...  21.3 us
    unnamed x2, local copies, waits for them, and re-layouts  2.6 us

profile of v2, /device:TPU:1, one launch (start us, length us, event | category | flops | bytes accessed | tf_op | source)
XLA Modules:
  0.0 26.9 jit_solution(17061667367711654233)
XLA Ops:
  1.3 21.3 %advance.1 = (f32[3,1,768]{2,1,0:T(1,128)}, s32[3,1,768]{2,1,0:T(1,128)}, s32[1,1]{1,0:T(1,128)}) custom-call(bf16[3,75,32,256]{3,2,1,0:T(8,128)(2,1)} %vel_hbm.1, f32[3,1,768]{2,1,0:T(1,128)} %off_hbm.1, s32[3,1,768]{2,1,0:T(1,128)} %cell_hbm.1, s32[1,1]{1,0:T(1,128)S(6)} %copy.11.count_smem, s32[1,768]{1,0:T(1,128)} %move_hbm.1), custom_call_target="tpu_custom_call" | custom-call | tf_op jit(solution)/shard_map/advance/pallas_call | solution.py:436
  22.6 1.3 %copy.12 = f32[3,1,768]{2,1,0:T(1,128)} copy(f32[3,1,768]{2,1,0:T(1,128)} %get-tuple-element.6) | data formatting | bytes 18432
  23.9 1.3 %copy.13 = s32[3,1,768]{2,1,0:T(1,128)} copy(s32[3,1,768]{2,1,0:T(1,128)} %get-tuple-element.7) | data formatting | bytes 18432

commit v3 on v2

--- a/solution.py
+++ b/solution.py
@@ -49,9 +49,9 @@
 
 
 def kernel(
-    dims, vel_hbm, off_hbm, cell_hbm, count_smem, move_hbm,
-    new_off, new_cell, new_count,
-    vel, off_ref, cell_ref, move_ref, table, where_ref, where_smem, gathered, posit, stay_ref, leave_ref,
+    dims, vel_hbm, off_hbm, cell_hbm, count_hbm, move_hbm,
+    out_ref,
+    vel, off_ref, cell_ref, move_ref, count_ref, table, where_ref, where_smem, gathered, posit, stay_ref, leave_ref,
     side, column, nrow, nfold, col_in, nrow_in, cnr_in,
     pack, pack_in, vsem, isem, send, recv, lsem, asem,
 ):
@@ -68,7 +68,7 @@
     top = r == n_lat - 1
     away = jnp.logical_and(top, corner != p)
 
-    smalls = [(cell_hbm, cell_ref), (move_hbm, move_ref), (off_hbm, off_ref)]
+    smalls = [(cell_hbm, cell_ref), (move_hbm, move_ref), (count_hbm, count_ref), (off_hbm, off_ref)]
     smalls = [pltpu.make_async_copy(src, dst, isem.at[n]) for n, (src, dst) in enumerate(smalls)]
     smalls[0].start()
     loads = [pltpu.make_async_copy(vel_hbm.at[c], vel.at[c], vsem.at[c]) for c in range(3)]
@@ -202,12 +202,12 @@
 
     def gather(step, carry):
         base = (step & 1) * half
-        group = step // 2
+        group = step >> 1
         ahead = lane - base
         accs = [gathered[n, group] for n in range(4)]
         for u in range(half):
             word = where_smem[step, u]
-            at, shift = word // LANES, word & (LANES - 1)
+            at, shift = word >> 7, word & (LANES - 1)
             here = ahead == u
             there = ahead == u + 1 if u < half - 1 else lane == ((base + half) & (LANES - 1))
             for dk in range(2):
@@ -221,7 +221,7 @@
     lax.fori_loop(0, live // half, gather, 0)
 
     motion = move_ref[:, 0:wide]
-    valid = iota((1, wide), 1) < count_smem[0, 0]
+    valid = iota((1, wide), 1) < count_ref[...]
     chosen = jnp.where((sub == motion) & valid, 1.0, 0.0)
     before = jnp.where(iota((LANES, LANES), 0) < iota((LANES, LANES), 1), 1.0, 0.0).astype(BF16)
     upto = jnp.concatenate([before, jnp.ones((LANES, LANES), BF16)], axis=1)
@@ -395,13 +395,7 @@
         filled = filled + jnp.sum(present, axis=1, keepdims=True)
     joined = placed(arrivals, slots_of(jnp.concatenate(targets, axis=1).astype(I32), slots))
     result = joined + jnp.concatenate([kept, jnp.zeros((8, slots - wide), F32)], axis=1)
-    decoded = jnp.maximum(result[3:4].astype(I32) - 1, 0)
-    for n in range(3):
-        new_off[n] = result[n : n + 1]
-    new_cell[0] = decoded & (cols - 1)
-    new_cell[1] = (decoded // cols) & (rows - 1)
-    new_cell[2] = decoded // (cols * rows)
-    new_count[...] = filled[:, 0:1].astype(I32)
+    out_ref[...] = jnp.where(iota((8, slots), 0) == 4, filled[:, 0:1], result)
 
     col_out.wait_send()
     east_out.wait_send()
@@ -421,6 +415,16 @@
     @pl.when(away)
     def _():
         cfold_out.wait_send()
+
+
+def decode(rows, cols, result_ref, new_off, new_cell, new_count):
+    for n in range(3):
+        new_off[n] = result_ref[n : n + 1, :]
+    code = jnp.maximum(result_ref[3:4, :].astype(I32) - 1, 0)
+    new_cell[0] = code & (cols - 1)
+    new_cell[1] = (code // cols) & (rows - 1)
+    new_cell[2] = code // (cols * rows)
+    new_count[...] = result_ref[4:5, 0:1].astype(I32)
 
 
 def shards(velocity, offsets, cells, counts, moves):
@@ -432,21 +436,21 @@
     dims = (depth, rows, cols, slots, live, lax.axis_size("lat"), lax.axis_size("lon"))
     groups = pl.cdiv(depth * rows, 8 * LANES) * 8
     vmem = pl.BlockSpec(memory_space=pltpu.VMEM)
-    hbm = pl.BlockSpec(memory_space=pl.ANY)
-    return pl.pallas_call(
+    hbm = pl.BlockSpec(memory_space=pltpu.HBM)
+    velocity, offsets, cells, moves = (
+        pltpu.with_memory_space_constraint(x, pltpu.HBM) for x in (velocity, offsets, cells, moves)
+    )
+    result = pl.pallas_call(
         functools.partial(kernel, dims),
-        out_shape=(
-            jax.ShapeDtypeStruct((3, 1, slots), F32),
-            jax.ShapeDtypeStruct((3, 1, slots), I32),
-            jax.ShapeDtypeStruct((1, 1), I32),
-        ),
-        in_specs=[hbm, hbm, hbm, pl.BlockSpec(memory_space=pltpu.SMEM), hbm],
-        out_specs=(vmem, vmem, vmem),
+        out_shape=jax.ShapeDtypeStruct((8, slots), F32),
+        in_specs=[hbm] * 5,
+        out_specs=vmem,
         scratch_shapes=[
             pltpu.VMEM((3, depth, rows, cols), BF16),
             pltpu.VMEM((3, 1, slots), F32),
             pltpu.VMEM((3, 1, slots), I32),
             pltpu.VMEM((1, slots), I32),
+            pltpu.VMEM((1, 1), I32),
             pltpu.VMEM((2 * deep * rows * 4, LANES), F32),
             pltpu.VMEM((2 * wide // LANES, LANES), I32),
             pltpu.SMEM((2 * wide // LANES, LANES), I32),
@@ -464,17 +468,29 @@
             pltpu.VMEM((4, 8, LANES), F32),
             pltpu.VMEM((4, 8, LANES), F32),
             pltpu.SemaphoreType.DMA((3,)),
-            pltpu.SemaphoreType.DMA((3,)),
+            pltpu.SemaphoreType.DMA((4,)),
             pltpu.SemaphoreType.DMA((9,)),
             pltpu.SemaphoreType.DMA((7,)),
             pltpu.SemaphoreType.DMA,
             pltpu.SemaphoreType.DMA,
         ],
         compiler_params=pltpu.CompilerParams(
-            collective_id=0, has_side_effects=True, vmem_limit_bytes=67043328
+            collective_id=0, has_side_effects=True, vmem_limit_bytes=32 * 1024 * 1024
         ),
         name="advance",
     )(velocity, offsets, cells, counts, moves)
+    return pl.pallas_call(
+        functools.partial(decode, rows, cols),
+        out_shape=(
+            jax.ShapeDtypeStruct((3, 1, slots), F32),
+            jax.ShapeDtypeStruct((3, 1, slots), I32),
+            jax.ShapeDtypeStruct((1, 1), I32),
+        ),
+        in_specs=[vmem],
+        out_specs=(vmem, vmem, vmem),
+        compiler_params=pltpu.CompilerParams(vmem_limit_bytes=1024 * 1024),
+        name="decode",
+    )(result)
 
 
 def solution(mesh):

time: 27.2 us -> 22.5 us (0.83)
  local copies, waits for them, and re-layouts: 2.6 us -> 0 us
  between operations: 3.05 us -> 1.29 us
    unnamed x2 -> x0, local copies, waits for them, and re-layouts: 2.6 us -> none
    pallas_call x1 -> x2, Pallas kernels: 21.3 us -> 21.1 us  [the longest x1 20.5 us: shards(): pl.pallas_call(functools.partial(kernel, dims), out_shape=jax.ShapeDtypeS...]
where the time goes in v3:
time: 22.5 us; the launch traced here: 22.4 us
  Pallas kernels  21.1 us (94%)
  between operations  1.29 us (6%)
    pallas_call x1, Pallas kernels, shards(): pl.pallas_call(functools.partial(kernel, dims), out_shape=jax.ShapeDtypeS...  20.5 us
    pallas_call x1, Pallas kernels, shards(): pl.pallas_call(functools.partial(decode, rows, cols), out_shape=(jax.Shap...  0.61 us

profile of v3, /device:TPU:1, one launch (start us, length us, event | category | flops | bytes accessed | tf_op | source)
XLA Modules:
  0.0 22.4 jit_solution(1068957258818208052)
XLA Ops:
  1.3 20.5 %advance.1.result_ref = f32[8,768]{1,0:T(8,128)S(1)} custom-call(bf16[3,75,32,256]{3,2,1,0:T(8,128)(2,1)} %vel_hbm.1, f32[3,1,768]{2,1,0:T(1,128)} %off_hbm.1, s32[3,1,768]{2,1,0:T(1,128)} %cell_hbm.1, s32[1,1]{1,0:T(1,128)S(6)} %copy.8.count_hbm, s32[1,768]{1,0:T(1,128)} %move_hbm.1), custom_call_target="tpu_custom_call" | custom-call | tf_op jit(solution)/shard_map/advance/pallas_call | solution.py:443
  21.8 0.6 %decode.1 = (f32[3,1,768]{2,1,0:T(1,128)}, s32[3,1,768]{2,1,0:T(1,128)}, s32[1,1]{1,0:T(1,128)}) custom-call(f32[8,768]{1,0:T(8,128)S(1)} %advance.1.result_ref), custom_call_target="tpu_custom_call" | custom-call | tf_op jit(solution)/shard_map/decode/pallas_call | solution.py:482

commit v4 on v3

v4 whole, which is shorter than its diff:
```python
import functools

import jax
import jax.numpy as jnp
from jax import lax
from jax.experimental import pallas as pl
from jax.experimental.pallas import tpu as pltpu
from jax.sharding import PartitionSpec as P

MESH = pl.DeviceIdType.MESH
CAP = 48
LANES = 128
F32, BF16, I32 = jnp.float32, jnp.bfloat16, jnp.int32
NT = (((1,), (1,)), ((), ()))
TN = (((0,), (0,)), ((), ()))


def iota(shape, dim):
    return lax.broadcasted_iota(I32, shape, dim)


def thirds(x):
    high = x.astype(BF16)
    rest = x - high.astype(F32)
    mid = rest.astype(BF16)
    low = (rest - mid.astype(F32)).astype(BF16)
    return jnp.concatenate([high.astype(F32), mid.astype(F32), low.astype(F32)], axis=0).astype(BF16)


def slots_of(target, size):
    return jnp.where(iota((size, target.shape[1]), 0) == target, 1.0, 0.0).astype(BF16)


def placed(records, onehot):
    out = lax.dot_general(thirds(records), onehot, NT, preferred_element_type=F32)
    return out[0:8] + out[8:16] + out[16:24]


def velocity_at(corners, a_row, b_row, c_row):
    sub = iota((8, a_row.shape[1]), 0)
    wb = jnp.where(sub < 4, 1.0 - b_row, b_row)
    w0 = (wb * (1.0 - c_row)).astype(BF16).astype(F32)
    w1 = (wb * c_row).astype(BF16).astype(F32)
    sums = []
    for d in range(2):
        s = w0 * corners[0][d] + w1 * corners[1][d]
        sums.append(s + pltpu.roll(s, 4, 0))
    return (1.0 - a_row) * sums[0] + a_row * sums[1]


def halo_corners(w, i_row, j_row, k_row, inside, top, sides, nrow_in, cnr_in):
    cols, rows = 2 * LANES, sides[0].shape[0]
    deep = (nrow_in.shape[0] - 16) // 2
    groups = sides[0].shape[1] // 8
    per = LANES // rows
    sub2 = iota((8, 2 * w), 0)

    def twice(x):
        return jnp.concatenate([x] * 2, axis=1)

    def hot(size, at):
        return jnp.where(iota((size, 2 * w), 0) == at, 1.0, 0.0).astype(BF16)

    k2 = jnp.concatenate([k_row, k_row + 1], axis=1)
    j2 = twice(j_row)
    outer = twice(jnp.where(i_row == cols - 1, groups, 0))
    at_side = hot(8 * groups, (k2 & (per - 1)) * (2 * groups) + outer + lax.shift_right_logical(k2, per.bit_length() - 1))
    base = twice(jnp.where(top, cols - 1 - i_row, i_row))
    second = base >= LANES
    inner = base & (LANES - 1)
    at_row = hot(2 * deep, k2 + jnp.where(second, deep, 0))
    at_level = hot(LANES, k2)

    eastern = jnp.zeros((8, 2 * w), F32)
    hits = [iota((rows, 2 * w), 0) == j2 + dj for dj in range(2)]
    for c in range(3):
        found = jnp.dot(sides[c], at_side, preferred_element_type=F32)
        for dj in range(2):
            value = jnp.sum(jnp.where(hits[dj], found, 0.0), axis=0, keepdims=True)
            eastern = jnp.where(sub2 == 4 * dj + c, value, eastern)

    few = jnp.concatenate([cnr_in[...], nrow_in[2 * deep :, 0:LANES].astype(F32)], axis=0).astype(BF16)
    ends = jnp.dot(few, at_level, preferred_element_type=F32)
    last = pltpu.roll(jnp.where(second, ends[0:8], ends[8:16]), 4, 0)

    pair = [jnp.zeros((8, 2 * w), F32), last]
    lane_id = iota((LANES, 2 * w), 0)
    hits = [lane_id == inner, lane_id == inner + 1]
    for c in range(3):
        found = lax.dot_general(
            nrow_in[0 : 2 * deep, c * LANES : (c + 1) * LANES], at_row, TN, preferred_element_type=F32
        )
        for d in range(2):
            value = jnp.sum(jnp.where(hits[d], found, 0.0), axis=0, keepdims=True)
            put = sub2 == 4 + c
            pair[d] = jnp.where(put & (inner < LANES - 1) if d else put, value, pair[d])

    sign = jnp.where(top, -1.0, 1.0)
    north = [sign * jnp.where(top, pair[1 - d], pair[d]) for d in range(2)]
    lower = iota((8, w), 0) >= 4
    corners = []
    for dk in range(2):
        part = slice(dk * w, (dk + 1) * w)
        out = []
        for d in range(2):
            here = inside[dk][d]
            if d == 1:
                here = jnp.where((i_row & (LANES - 1)) == LANES - 1, eastern[:, part], here)
            out.append(jnp.where(lower & (j_row == rows - 1), north[d][:, part], here))
        corners.append(out)
    return corners


def advanced(corners, position):
    first = velocity_at(corners, position[0:1], position[1:2], position[2:3])
    middle = position + 0.5 * first
    return position + velocity_at(corners, middle[0:1], middle[1:2], middle[2:3])


def kernel(
    dims, vel_hbm, off_hbm, cell_hbm, count_hbm, move_hbm,
    out_ref,
    vel, off_ref, cell_ref, move_ref, count_ref, table, where_ref, where_smem, first_ref, first_smem,
    gathered, first_gathered, stay_ref,
    side, column, nrow, nfold, cnr, cfold, col_in, nrow_in, cnr_in,
    pack, pack_in, vsem, isem, send, recv, lsem, asem,
):
    depth, rows, cols, slots, live, n_lat, n_lon = dims
    wide = pl.cdiv(live, LANES) * LANES
    tiles = wide // LANES
    half = LANES // 2
    few = 4 * half
    level = rows * 4
    span = table.shape[0] // 2
    deep = span // level
    per = LANES // rows
    groups = side.shape[1]
    r, p = lax.axis_index("lat"), lax.axis_index("lon")
    east, west = lax.rem(p + 1, n_lon), lax.rem(p + n_lon - 1, n_lon)
    across, corner = n_lon - 1 - p, lax.rem(n_lon - p, n_lon)
    top = r == n_lat - 1
    away = jnp.logical_and(top, corner != p)

    smalls = [(cell_hbm, cell_ref), (move_hbm, move_ref), (count_hbm, count_ref), (off_hbm, off_ref)]
    smalls = [pltpu.make_async_copy(src, dst, isem.at[n]) for n, (src, dst) in enumerate(smalls)]
    for small in smalls:
        small.start()
    loads = [pltpu.make_async_copy(vel_hbm.at[c], vel.at[c], vsem.at[c]) for c in range(3)]
    for load in loads:
        load.start()

    barrier = pltpu.get_barrier_semaphore()

    def greet(lat, lon):
        pl.semaphore_signal(barrier, inc=1, device_id=(lon, lat), device_id_type=MESH)

    greet(r, east)
    greet(r, west)

    @pl.when(r < n_lat - 1)
    def _():
        greet(r + 1, p)
        greet(r + 1, east)

    @pl.when(r > 0)
    def _():
        greet(r - 1, p)

    @pl.when(top)
    def _():
        greet(r, across)

    @pl.when(away)
    def _():
        greet(r, corner)

    lane = iota((8, LANES), 1)
    sub = iota((8, wide), 0)
    for small in smalls:
        small.wait()

    i_row, j_row, k_row = (cell_ref[n, :, 0:wide] for n in range(3))
    motion = move_ref[:, 0:wide]
    valid = iota((1, wide), 1) < count_ref[...]
    chosen = jnp.where((sub == motion) & valid, 1.0, 0.0)
    before = jnp.where(iota((LANES, LANES), 0) < iota((LANES, LANES), 1), 1.0, 0.0).astype(BF16)
    upto = jnp.concatenate([before, jnp.ones((LANES, LANES), BF16)], axis=1)

    def ranked(flags, total):
        out = []
        for t in range(flags.shape[1] // LANES):
            sums = jnp.dot(
                flags[:, t * LANES : (t + 1) * LANES].astype(BF16), upto, preferred_element_type=F32
            )
            out.append(sums[:, :LANES] + total)
            total = total + sums[:, LANES:]
        return jnp.concatenate(out, axis=1), total

    rank, total = ranked(chosen, jnp.zeros((8, LANES), F32))
    stay_to = jnp.where(chosen[0:1] > 0.5, rank[0:1], -1.0).astype(I32)
    slot_to = rank + (half * (sub - 1)).astype(F32)
    leaving = (sub >= 1) & (chosen > 0.5)
    leave_to = (jnp.sum(jnp.where(leaving, slot_to + 1.0, 0.0), axis=0, keepdims=True) - 1.0).astype(I32)
    position = jnp.zeros((8, wide), F32)
    for n in range(3):
        position = jnp.where(sub == n, off_ref[n, :, 0:wide], position)
    marks = jnp.where(sub == 0, i_row, jnp.where(sub == 1, j_row, jnp.where(sub == 2, k_row, 1)))
    raw = lax.dot_general(
        jnp.concatenate([thirds(position).astype(F32), marks.astype(F32)], axis=0).astype(BF16),
        slots_of(leave_to, few), NT, preferred_element_type=F32,
    )
    first_position = raw[0:8] + raw[8:16] + raw[16:24]
    first_i, first_j, first_k = (
        jnp.clip(raw[24 + n : 25 + n].astype(I32), 0, top_value)
        for n, top_value in enumerate((cols - 1, rows - 1, depth - 2))
    )
    first_real = raw[27:28] > 0.5

    def words(i, j, k, target):
        start = jnp.where(i >= LANES, span, 0) + k * level + 4 * j
        start = start * LANES + ((iota(i.shape, 1) - i) & (LANES - 1))
        for t in range(i.shape[1] // LANES):
            part = start[:, t * LANES : (t + 1) * LANES]
            target[2 * t : 2 * t + 1, :] = part
            target[2 * t + 1 : 2 * t + 2, :] = pltpu.roll(part, half, 1)

    words(first_i, first_j, first_k, first_ref)
    words(i_row, j_row, k_row, where_ref)
    addresses = [
        pltpu.make_async_copy(first_ref, first_smem, asem.at[0]),
        pltpu.make_async_copy(where_ref, where_smem, asem.at[1]),
    ]
    for copy in addresses:
        copy.start()
    stay_ref[...] = slots_of(stay_to, wide)

    for part in range(2):
        table[pl.ds(part * span + depth * level, span - depth * level), :] = jnp.zeros(
            (span - depth * level, LANES), F32
        )
    side[...] = jnp.zeros_like(side)
    gathered[...] = jnp.zeros_like(gathered)
    first_gathered[...] = jnp.zeros_like(first_gathered)
    first_lane = jnp.where(lane == 0, 1.0, 0.0).astype(BF16)
    for c in range(3):
        loads[c].wait()

        def build(step, carry):
            for u in range(5):
                k = step * 5 + u
                for h in range(2):
                    plane = vel[c, k, :, h * LANES : (h + 1) * LANES].astype(F32)
                    for s in range(rows // 8):
                        at = h * span + k * level + 32 * s + c
                        table[pl.ds(at, 8, stride=4), :] = plane[8 * s : 8 * s + 8]
            return carry

        lax.fori_loop(0, depth // 5, build, 0)

        for h in range(2):
            plane = vel[c, :, :, h * LANES : (h + 1) * LANES].reshape(depth * rows, LANES)
            line = lax.dot_general(first_lane, plane, NT, preferred_element_type=F32)[0:1]
            for g in range(pl.cdiv(depth, per)):
                n = min(LANES, depth * rows - g * LANES)
                side[h * 3 + c, g : g + 1, 0:n] = line[:, g * LANES : g * LANES + n]
    column[...] = side[0:3].astype(BF16)

    def edge(target, ends, row):
        firsts = [jnp.zeros((8, deep), F32)] * 2
        for h in range(2):
            for c in range(3):
                blocks = []
                for block in range(deep // 8):
                    at = h * span + block * 8 * level + 4 * row + c
                    blocks.append(table[pl.ds(at, 8, stride=level), :])
                plane = jnp.concatenate(blocks, axis=0).astype(BF16)
                target[pl.ds(h * deep, deep), pl.ds(c * LANES, LANES)] = plane
                pick = jnp.where((lane == 0) & (iota((8, LANES), 0) == c), 1.0, 0.0).astype(BF16)
                firsts[h] = firsts[h] + lax.dot_general(pick, plane, NT, preferred_element_type=F32)
        pad = jnp.zeros((8, LANES - deep), F32)
        tail = jnp.concatenate([jnp.concatenate([firsts[1], pad], axis=1), jnp.zeros((8, LANES), F32)], axis=0)
        target[2 * deep : 2 * deep + 16, :] = jnp.concatenate([tail, jnp.zeros((16, 2 * LANES), F32)], axis=1).astype(BF16)
        ends[...] = jnp.concatenate([firsts[0], pad], axis=1)

    edge(nrow, cnr, 0)

    @pl.when(top)
    def _():
        edge(nfold, cfold, rows - 1)

    def remote(src, dst, s, t, lat, lon):
        return pltpu.make_async_remote_copy(
            src, dst, send.at[s], recv.at[t], device_id=(lon, lat), device_id_type=MESH
        )

    col_out = remote(column, col_in, 0, 0, r, west)
    row_out = remote(nrow, nrow_in, 1, 1, r - 1, p)
    cnr_out = remote(cnr, cnr_in, 2, 2, r - 1, west)
    fold_out = remote(nfold, nrow_in, 3, 1, r, across)
    cfold_out = remote(cfold, cnr_in, 4, 2, r, corner)
    cfold_here = pltpu.make_async_copy(cfold, cnr_in, lsem)

    peers = 2 + 2 * (r > 0).astype(I32) + (r < n_lat - 1).astype(I32) + top.astype(I32) + away.astype(I32)
    pl.semaphore_wait(barrier, peers)

    @pl.when(r > 0)
    def _():
        row_out.start()
        cnr_out.start()

    @pl.when(top)
    def _():
        fold_out.start()

    @pl.when(away)
    def _():
        cfold_out.start()

    @pl.when(jnp.logical_and(top, corner == p))
    def _():
        cfold_here.start()

    col_out.start()

    def gather(source, target, count):
        def body(step, carry):
            base = (step & 1) * half
            group = step >> 1
            ahead = lane - base
            accs = [target[n, group] for n in range(4)]
            for u in range(count):
                word = source[step, u]
                at, shift = word >> 7, word & (LANES - 1)
                here = ahead == u
                there = ahead == u + 1 if u < half - 1 else lane == ((base + half) & (LANES - 1))
                for dk in range(2):
                    turned = pltpu.roll(table[pl.ds(at + dk * level, 8), :], shift, 1)
                    accs[2 * dk] = jnp.where(here, turned, accs[2 * dk])
                    accs[2 * dk + 1] = jnp.where(there, turned, accs[2 * dk + 1])
            for n in range(4):
                target[n, group] = accs[n]
            return carry

        return body

    def together(source, w):
        out = []
        for dk in range(2):
            low = [source[2 * dk, t] for t in range(w // LANES)]
            high = [pltpu.roll(source[2 * dk + 1, t], LANES - 1, 1) for t in range(w // LANES)]
            out.append([jnp.concatenate(low, axis=1), jnp.concatenate(high, axis=1)])
        return out

    addresses[0].wait()
    lax.fori_loop(0, 4, gather(first_smem, first_gathered, CAP), 0)
    addresses[1].wait()

    go = iota((1, few), 1) // half + 1
    folding = (go == 3) & top
    last_i, last_j = cols - 1, rows - 1
    new_i = jnp.where(
        go == 1, 0, jnp.where(go == 2, last_i, jnp.where(folding, last_i - first_i, first_i))
    )
    new_j = jnp.where(
        go == 3, jnp.where(top, last_j, 0), jnp.where(go == 4, last_j, first_j)
    )
    code = jnp.where(first_real, 1 + new_i + cols * (new_j + rows * first_k), 0).astype(F32)

    cnr_wait = remote(cnr, cnr_in, 2, 2, r, west)
    col_out.wait_recv()
    row_out.wait_recv()

    @pl.when(jnp.logical_or(jnp.logical_not(top), corner != p))
    def _():
        cnr_wait.wait_recv()

    @pl.when(jnp.logical_and(top, corner == p))
    def _():
        cfold_here.wait()

    sides = []
    for c in range(3):
        lines = jnp.concatenate([side[3 + c], col_in[c].astype(F32)], axis=0)
        lines = [lines if m == 0 else pltpu.roll(lines, LANES - m * rows, 1) for m in range(per)]
        sides.append(jnp.concatenate(lines, axis=0).T[0:rows].astype(BF16))

    corners = halo_corners(
        few, first_i, first_j, first_k, together(first_gathered, few), top, sides, nrow_in, cnr_in
    )
    moved = advanced(corners, first_position)
    na, nb, nc = moved[0:1], moved[1:2], moved[2:3]
    new_a = jnp.where(go == 1, na - 1.0, jnp.where(go == 2, na + 1.0, jnp.where(folding, 1.0 - na, na)))
    new_b = jnp.where(go == 3, jnp.where(top, 2.0 - nb, nb - 1.0), jnp.where(go == 4, nb + 1.0, nb))
    sub_few = iota((8, few), 0)
    records = jnp.where(
        sub_few == 0, new_a,
        jnp.where(sub_few == 1, new_b, jnp.where(sub_few == 2, nc, jnp.where(sub_few == 3, code, 0.0))),
    )
    records = jnp.where(first_real, records, 0.0)

    for m in range(2):
        pack[m] = records[:, m * LANES : (m + 1) * LANES]

    @pl.when(r == 0)
    def _():
        pack_in[2] = jnp.zeros((8, LANES), F32)

    east_out = remote(pack.at[0], pack_in.at[0], 5, 3, r, east)
    west_out = remote(pack.at[0], pack_in.at[1], 6, 4, r, west)
    north_out = remote(pack.at[1], pack_in.at[2], 7, 5, r + 1, p)
    over_out = remote(pack.at[1], pack_in.at[3], 7, 6, r, across)
    south_out = remote(pack.at[1], pack_in.at[3], 8, 6, r - 1, p)

    @pl.when(top)
    def _():
        over_out.start()

    @pl.when(r < n_lat - 1)
    def _():
        north_out.start()

    @pl.when(r > 0)
    def _():
        south_out.start()

    east_out.start()
    west_out.start()

    lax.fori_loop(0, live // half, gather(where_smem, gathered, half), 0)
    corners = halo_corners(
        wide, i_row, j_row, k_row, together(gathered, wide), top, sides, nrow_in, cnr_in
    )
    moved = advanced(corners, position)
    code = (1 + i_row + cols * (j_row + rows * k_row)).astype(F32)
    kept = placed(jnp.where(sub < 3, moved, jnp.where(sub == 3, code, 0.0)), stay_ref[...])

    east_out.wait_recv()
    west_out.wait_recv()

    @pl.when(r > 0)
    def _():
        north_out.wait_recv()

    over_out.wait_recv()

    from_north = jnp.where(top, pltpu.roll(pack_in[3], half, 1), pack_in[3])
    arrivals = jnp.concatenate(
        [
            jnp.where(lane < half, pack_in[0], pack_in[1]),
            jnp.where(lane < half, pack_in[2], from_north),
        ],
        axis=1,
    )
    present = jnp.where(arrivals > 0.5, 1.0, 0.0)
    order, filled = ranked(present, jnp.broadcast_to(total[0:1], (8, LANES)))
    arrive_to = jnp.where(present[3:4] > 0.5, order[3:4], -1.0).astype(I32)
    joined = placed(arrivals, slots_of(arrive_to, slots))
    result = joined + jnp.concatenate([kept, jnp.zeros((8, slots - wide), F32)], axis=1)
    out_ref[...] = jnp.where(iota((8, slots), 0) == 4, filled[3:4, 0:1], result)

    col_out.wait_send()
    east_out.wait_send()
    west_out.wait_send()
    north_out.wait_send()

    @pl.when(r > 0)
    def _():
        row_out.wait_send()
        cnr_out.wait_send()
        south_out.wait_send()

    @pl.when(top)
    def _():
        fold_out.wait_send()

    @pl.when(away)
    def _():
        cfold_out.wait_send()


def decode(rows, cols, result_ref, new_off, new_cell, new_count):
    for n in range(3):
        new_off[n] = result_ref[n : n + 1, :]
    code = jnp.maximum(result_ref[3:4, :].astype(I32) - 1, 0)
    new_cell[0] = code & (cols - 1)
    new_cell[1] = (code // cols) & (rows - 1)
    new_cell[2] = code // (cols * rows)
    new_count[...] = result_ref[4:5, 0:1].astype(I32)


def shards(velocity, offsets, cells, counts, moves):
    _, depth, rows, cols = velocity.shape
    slots = offsets.shape[2]
    live = slots * 3 // 4
    wide = pl.cdiv(live, LANES) * LANES
    deep = pl.cdiv(depth, 16) * 16
    dims = (depth, rows, cols, slots, live, lax.axis_size("lat"), lax.axis_size("lon"))
    groups = pl.cdiv(depth * rows, 8 * LANES) * 8
    vmem = pl.BlockSpec(memory_space=pltpu.VMEM)
    hbm = pl.BlockSpec(memory_space=pltpu.HBM)
    velocity, offsets, cells, moves = (
        pltpu.with_memory_space_constraint(x, pltpu.HBM) for x in (velocity, offsets, cells, moves)
    )
    result = pl.pallas_call(
        functools.partial(kernel, dims),
        out_shape=jax.ShapeDtypeStruct((8, slots), F32),
        in_specs=[hbm] * 5,
        out_specs=vmem,
        scratch_shapes=[
            pltpu.VMEM((3, depth, rows, cols), BF16),
            pltpu.VMEM((3, 1, slots), F32),
            pltpu.VMEM((3, 1, slots), I32),
            pltpu.VMEM((1, slots), I32),
            pltpu.VMEM((1, 1), I32),
            pltpu.VMEM((2 * deep * rows * 4, LANES), F32),
            pltpu.VMEM((2 * wide // LANES, LANES), I32),
            pltpu.SMEM((2 * wide // LANES, LANES), I32),
            pltpu.VMEM((4, LANES), I32),
            pltpu.SMEM((4, LANES), I32),
            pltpu.VMEM((4, wide // LANES, 8, LANES), F32),
            pltpu.VMEM((4, 2, 8, LANES), F32),
            pltpu.VMEM((wide, wide), BF16),
            pltpu.VMEM((6, groups, LANES), F32),
            pltpu.VMEM((3, groups, LANES), BF16),
            pltpu.VMEM((2 * deep + 16, 3 * LANES), BF16),
            pltpu.VMEM((2 * deep + 16, 3 * LANES), BF16),
            pltpu.VMEM((8, LANES), F32),
            pltpu.VMEM((8, LANES), F32),
            pltpu.VMEM((3, groups, LANES), BF16),
            pltpu.VMEM((2 * deep + 16, 3 * LANES), BF16),
            pltpu.VMEM((8, LANES), F32),
            pltpu.VMEM((2, 8, LANES), F32),
            pltpu.VMEM((4, 8, LANES), F32),
            pltpu.SemaphoreType.DMA((3,)),
            pltpu.SemaphoreType.DMA((4,)),
            pltpu.SemaphoreType.DMA((9,)),
            pltpu.SemaphoreType.DMA((7,)),
            pltpu.SemaphoreType.DMA,
            pltpu.SemaphoreType.DMA((2,)),
        ],
        compiler_params=pltpu.CompilerParams(
            collective_id=0, has_side_effects=True, vmem_limit_bytes=32 * 1024 * 1024
        ),
        name="advance",
    )(velocity, offsets, cells, counts, moves)
    return pl.pallas_call(
        functools.partial(decode, rows, cols),
        out_shape=(
            jax.ShapeDtypeStruct((3, 1, slots), F32),
            jax.ShapeDtypeStruct((3, 1, slots), I32),
            jax.ShapeDtypeStruct((1, 1), I32),
        ),
        in_specs=[vmem],
        out_specs=(vmem, vmem, vmem),
        compiler_params=pltpu.CompilerParams(vmem_limit_bytes=1024 * 1024),
        name="decode",
    )(result)


def solution(mesh):
    placed_in = (
        P(None, None, "lat", "lon"),
        P(None, "lat", "lon"),
        P(None, "lat", "lon"),
        P("lat", "lon"),
        P("lat", "lon"),
    )
    return jax.shard_map(
        shards,
        mesh=mesh,
        in_specs=placed_in,
        out_specs=(P(None, "lat", "lon"), P(None, "lat", "lon"), P("lat", "lon")),
        check_vma=False,
    )
```

time: 22.5 us -> 22.4 us (level); the launches traced: 22.4 us -> 22 us
  Pallas kernels: 21.1 us -> 20.7 us
    pallas_call x1, Pallas kernels: 20.5 us -> 20.1 us  [shards(): pl.pallas_call(functools.partial(kernel, dims), out_shape=jax.ShapeDtypeS...]
where the time goes in v4:
time: 22.4 us; the launch traced here: 22 us
  Pallas kernels  20.7 us (92%)
  between operations  1.29 us (6%)
    pallas_call x1, Pallas kernels, shards(): pl.pallas_call(functools.partial(kernel, dims), out_shape=jax.ShapeDtypeS...  20.1 us
    pallas_call x1, Pallas kernels, shards(): pl.pallas_call(functools.partial(decode, rows, cols), out_shape=(jax.Shap...  0.61 us

profile of v4, /device:TPU:1, one launch (start us, length us, event | category | flops | bytes accessed | tf_op | source)
XLA Modules:
  0.0 22.0 jit_solution(4937065314632702660)
XLA Ops:
  1.3 20.1 %advance.1.result_ref = f32[8,768]{1,0:T(8,128)S(1)} custom-call(bf16[3,75,32,256]{3,2,1,0:T(8,128)(2,1)} %vel_hbm.1, f32[3,1,768]{2,1,0:T(1,128)} %off_hbm.1, s32[3,1,768]{2,1,0:T(1,128)} %cell_hbm.1, s32[1,1]{1,0:T(1,128)S(6)} %copy.8.count_hbm, s32[1,768]{1,0:T(1,128)} %move_hbm.1), custom_call_target="tpu_custom_call" | custom-call | tf_op jit(solution)/shard_map/advance/pallas_call | solution.py:504
  21.4 0.6 %decode.1 = (f32[3,1,768]{2,1,0:T(1,128)}, s32[3,1,768]{2,1,0:T(1,128)}, s32[1,1]{1,0:T(1,128)}) custom-call(f32[8,768]{1,0:T(8,128)S(1)} %advance.1.result_ref), custom_call_target="tpu_custom_call" | custom-call | tf_op jit(solution)/shard_map/decode/pallas_call | solution.py:546

commit v5 on v4

--- a/solution.py
+++ b/solution.py
@@ -145,7 +145,12 @@
     smalls = [pltpu.make_async_copy(src, dst, isem.at[n]) for n, (src, dst) in enumerate(smalls)]
     for small in smalls:
         small.start()
-    loads = [pltpu.make_async_copy(vel_hbm.at[c], vel.at[c], vsem.at[c]) for c in range(3)]
+    bands = [slice(8 * n, 8 * n + 8) for n in range(rows // 8)]
+    bands = [bands[0], bands[-1]] + bands[1:-1]
+    loads = [
+        pltpu.make_async_copy(vel_hbm.at[:, :, band, :], vel.at[:, :, band, :], vsem.at[n])
+        for n, band in enumerate(bands)
+    ]
     for load in loads:
         load.start()
 
@@ -242,28 +247,21 @@
     gathered[...] = jnp.zeros_like(gathered)
     first_gathered[...] = jnp.zeros_like(first_gathered)
     first_lane = jnp.where(lane == 0, 1.0, 0.0).astype(BF16)
-    for c in range(3):
-        loads[c].wait()
-
-        def build(step, carry):
+
+    def build(n):
+        band = bands[n]
+        loads[n].wait()
+
+        def body(step, carry):
             for u in range(5):
                 k = step * 5 + u
-                for h in range(2):
-                    plane = vel[c, k, :, h * LANES : (h + 1) * LANES].astype(F32)
-                    for s in range(rows // 8):
-                        at = h * span + k * level + 32 * s + c
-                        table[pl.ds(at, 8, stride=4), :] = plane[8 * s : 8 * s + 8]
+                for c in range(3):
+                    for h in range(2):
+                        at = h * span + k * level + 4 * band.start + c
+                        table[pl.ds(at, 8, stride=4), :] = vel[c, k, band, h * LANES : (h + 1) * LANES].astype(F32)
             return carry
 
-        lax.fori_loop(0, depth // 5, build, 0)
-
-        for h in range(2):
-            plane = vel[c, :, :, h * LANES : (h + 1) * LANES].reshape(depth * rows, LANES)
-            line = lax.dot_general(first_lane, plane, NT, preferred_element_type=F32)[0:1]
-            for g in range(pl.cdiv(depth, per)):
-                n = min(LANES, depth * rows - g * LANES)
-                side[h * 3 + c, g : g + 1, 0:n] = line[:, g * LANES : g * LANES + n]
-    column[...] = side[0:3].astype(BF16)
+        lax.fori_loop(0, depth // 5, body, 0)
 
     def edge(target, ends, row):
         firsts = [jnp.zeros((8, deep), F32)] * 2
@@ -282,12 +280,6 @@
         target[2 * deep : 2 * deep + 16, :] = jnp.concatenate([tail, jnp.zeros((16, 2 * LANES), F32)], axis=1).astype(BF16)
         ends[...] = jnp.concatenate([firsts[0], pad], axis=1)
 
-    edge(nrow, cnr, 0)
-
-    @pl.when(top)
-    def _():
-        edge(nfold, cfold, rows - 1)
-
     def remote(src, dst, s, t, lat, lon):
         return pltpu.make_async_remote_copy(
             src, dst, send.at[s], recv.at[t], device_id=(lon, lat), device_id_type=MESH
@@ -300,6 +292,8 @@
     cfold_out = remote(cfold, cnr_in, 4, 2, r, corner)
     cfold_here = pltpu.make_async_copy(cfold, cnr_in, lsem)
 
+    build(0)
+    edge(nrow, cnr, 0)
     peers = 2 + 2 * (r > 0).astype(I32) + (r < n_lat - 1).astype(I32) + top.astype(I32) + away.astype(I32)
     pl.semaphore_wait(barrier, peers)
 
@@ -308,8 +302,11 @@
         row_out.start()
         cnr_out.start()
 
+    build(1)
+
     @pl.when(top)
     def _():
+        edge(nfold, cfold, rows - 1)
         fold_out.start()
 
     @pl.when(away)
@@ -320,6 +317,17 @@
     def _():
         cfold_here.start()
 
+    for n in range(2, len(bands)):
+        build(n)
+
+    for c in range(3):
+        for h in range(2):
+            plane = vel[c, :, :, h * LANES : (h + 1) * LANES].reshape(depth * rows, LANES)
+            line = lax.dot_general(first_lane, plane, NT, preferred_element_type=F32)[0:1]
+            for g in range(pl.cdiv(depth, per)):
+                n = min(LANES, depth * rows - g * LANES)
+                side[h * 3 + c, g : g + 1, 0:n] = line[:, g * LANES : g * LANES + n]
+    column[...] = side[0:3].astype(BF16)
     col_out.start()
 
     def gather(source, target, count):
@@ -351,9 +359,10 @@
             out.append([jnp.concatenate(low, axis=1), jnp.concatenate(high, axis=1)])
         return out
 
-    addresses[0].wait()
+    for copy in addresses:
+        copy.wait()
     lax.fori_loop(0, 4, gather(first_smem, first_gathered, CAP), 0)
-    addresses[1].wait()
+    lax.fori_loop(0, live // half, gather(where_smem, gathered, half), 0)
 
     go = iota((1, few), 1) // half + 1
     folding = (go == 3) & top
@@ -426,7 +435,6 @@
     east_out.start()
     west_out.start()
 
-    lax.fori_loop(0, live // half, gather(where_smem, gathered, half), 0)
     corners = halo_corners(
         wide, i_row, j_row, k_row, together(gathered, wide), top, sides, nrow_in, cnr_in
     )
@@ -531,7 +539,7 @@
             pltpu.VMEM((8, LANES), F32),
             pltpu.VMEM((2, 8, LANES), F32),
             pltpu.VMEM((4, 8, LANES), F32),
-            pltpu.SemaphoreType.DMA((3,)),
+            pltpu.SemaphoreType.DMA((rows // 8,)),
             pltpu.SemaphoreType.DMA((4,)),
             pltpu.SemaphoreType.DMA((9,)),
             pltpu.SemaphoreType.DMA((7,)),

time: 22.4 us -> 20.8 us (0.929)
  the two profiles are of different devices: /device:TPU:1 before, /device:TPU:6 now
where the time goes in v5:
time: 20.8 us; the launch traced here: 20.7 us
  Pallas kernels  19.4 us (93%)
  between operations  1.29 us (6%)
    pallas_call x1, Pallas kernels, shards(): pl.pallas_call(functools.partial(kernel, dims), out_shape=jax.ShapeDtypeS...  18.8 us
    pallas_call x1, Pallas kernels, shards(): pl.pallas_call(functools.partial(decode, rows, cols), out_shape=(jax.Shap...  0.61 us

profile of v5, /device:TPU:6, one launch (start us, length us, event | category | flops | bytes accessed | tf_op | source)
XLA Modules:
  0.0 20.7 jit_solution(10881230415879726177)
XLA Ops:
  1.3 18.8 %advance.1.result_ref = f32[8,768]{1,0:T(8,128)S(1)} custom-call(bf16[3,75,32,256]{3,2,1,0:T(8,128)(2,1)} %vel_hbm.1, f32[3,1,768]{2,1,0:T(1,128)} %off_hbm.1, s32[3,1,768]{2,1,0:T(1,128)} %cell_hbm.1, s32[1,1]{1,0:T(1,128)S(6)} %copy.8.count_hbm, s32[1,768]{1,0:T(1,128)} %move_hbm.1), custom_call_target="tpu_custom_call" | custom-call | tf_op jit(solution)/shard_map/advance/pallas_call | solution.py:512
  20.1 0.6 %decode.1 = (f32[3,1,768]{2,1,0:T(1,128)}, s32[3,1,768]{2,1,0:T(1,128)}, s32[1,1]{1,0:T(1,128)}) custom-call(f32[8,768]{1,0:T(8,128)S(1)} %advance.1.result_ref), custom_call_target="tpu_custom_call" | custom-call | tf_op jit(solution)/shard_map/decode/pallas_call | solution.py:554

commit v6 on v5

--- a/solution.py
+++ b/solution.py
@@ -143,16 +143,15 @@
 
     smalls = [(cell_hbm, cell_ref), (move_hbm, move_ref), (count_hbm, count_ref), (off_hbm, off_ref)]
     smalls = [pltpu.make_async_copy(src, dst, isem.at[n]) for n, (src, dst) in enumerate(smalls)]
-    for small in smalls:
-        small.start()
     bands = [slice(8 * n, 8 * n + 8) for n in range(rows // 8)]
     bands = [bands[0], bands[-1]] + bands[1:-1]
     loads = [
         pltpu.make_async_copy(vel_hbm.at[:, :, band, :], vel.at[:, :, band, :], vsem.at[n])
         for n, band in enumerate(bands)
     ]
-    for load in loads:
-        load.start()
+    loads[0].start()
+    for copy in smalls + loads[1:]:
+        copy.start()
 
     barrier = pltpu.get_barrier_semaphore()
 
@@ -181,64 +180,6 @@
 
     lane = iota((8, LANES), 1)
     sub = iota((8, wide), 0)
-    for small in smalls:
-        small.wait()
-
-    i_row, j_row, k_row = (cell_ref[n, :, 0:wide] for n in range(3))
-    motion = move_ref[:, 0:wide]
-    valid = iota((1, wide), 1) < count_ref[...]
-    chosen = jnp.where((sub == motion) & valid, 1.0, 0.0)
-    before = jnp.where(iota((LANES, LANES), 0) < iota((LANES, LANES), 1), 1.0, 0.0).astype(BF16)
-    upto = jnp.concatenate([before, jnp.ones((LANES, LANES), BF16)], axis=1)
-
-    def ranked(flags, total):
-        out = []
-        for t in range(flags.shape[1] // LANES):
-            sums = jnp.dot(
-                flags[:, t * LANES : (t + 1) * LANES].astype(BF16), upto, preferred_element_type=F32
-            )
-            out.append(sums[:, :LANES] + total)
-            total = total + sums[:, LANES:]
-        return jnp.concatenate(out, axis=1), total
-
-    rank, total = ranked(chosen, jnp.zeros((8, LANES), F32))
-    stay_to = jnp.where(chosen[0:1] > 0.5, rank[0:1], -1.0).astype(I32)
-    slot_to = rank + (half * (sub - 1)).astype(F32)
-    leaving = (sub >= 1) & (chosen > 0.5)
-    leave_to = (jnp.sum(jnp.where(leaving, slot_to + 1.0, 0.0), axis=0, keepdims=True) - 1.0).astype(I32)
-    position = jnp.zeros((8, wide), F32)
-    for n in range(3):
-        position = jnp.where(sub == n, off_ref[n, :, 0:wide], position)
-    marks = jnp.where(sub == 0, i_row, jnp.where(sub == 1, j_row, jnp.where(sub == 2, k_row, 1)))
-    raw = lax.dot_general(
-        jnp.concatenate([thirds(position).astype(F32), marks.astype(F32)], axis=0).astype(BF16),
-        slots_of(leave_to, few), NT, preferred_element_type=F32,
-    )
-    first_position = raw[0:8] + raw[8:16] + raw[16:24]
-    first_i, first_j, first_k = (
-        jnp.clip(raw[24 + n : 25 + n].astype(I32), 0, top_value)
-        for n, top_value in enumerate((cols - 1, rows - 1, depth - 2))
-    )
-    first_real = raw[27:28] > 0.5
-
-    def words(i, j, k, target):
-        start = jnp.where(i >= LANES, span, 0) + k * level + 4 * j
-        start = start * LANES + ((iota(i.shape, 1) - i) & (LANES - 1))
-        for t in range(i.shape[1] // LANES):
-            part = start[:, t * LANES : (t + 1) * LANES]
-            target[2 * t : 2 * t + 1, :] = part
-            target[2 * t + 1 : 2 * t + 2, :] = pltpu.roll(part, half, 1)
-
-    words(first_i, first_j, first_k, first_ref)
-    words(i_row, j_row, k_row, where_ref)
-    addresses = [
-        pltpu.make_async_copy(first_ref, first_smem, asem.at[0]),
-        pltpu.make_async_copy(where_ref, where_smem, asem.at[1]),
-    ]
-    for copy in addresses:
-        copy.start()
-    stay_ref[...] = slots_of(stay_to, wide)
-
     for part in range(2):
         table[pl.ds(part * span + depth * level, span - depth * level), :] = jnp.zeros(
             (span - depth * level, LANES), F32
@@ -295,23 +236,98 @@
     build(0)
     edge(nrow, cnr, 0)
     peers = 2 + 2 * (r > 0).astype(I32) + (r < n_lat - 1).astype(I32) + top.astype(I32) + away.astype(I32)
-    pl.semaphore_wait(barrier, peers)
-
-    @pl.when(r > 0)
-    def _():
-        row_out.start()
-        cnr_out.start()
+
+    def send_rows():
+        pl.semaphore_wait(barrier, peers)
+
+        @pl.when(r > 0)
+        def _():
+            cnr_out.start()
+            row_out.start()
+
+    def send_fold():
+        @pl.when(top)
+        def _():
+            fold_out.start()
+
+        @pl.when(away)
+        def _():
+            cfold_out.start()
+
+    patient = p == 0
+    eager = jnp.logical_not(patient)
+
+    @pl.when(eager)
+    def _():
+        send_rows()
+
+    for small in smalls:
+        small.wait()
+
+    i_row, j_row, k_row = (cell_ref[n, :, 0:wide] for n in range(3))
+    motion = move_ref[:, 0:wide]
+    valid = iota((1, wide), 1) < count_ref[...]
+    chosen = jnp.where((sub == motion) & valid, 1.0, 0.0)
+    before = jnp.where(iota((LANES, LANES), 0) < iota((LANES, LANES), 1), 1.0, 0.0).astype(BF16)
+    upto = jnp.concatenate([before, jnp.ones((LANES, LANES), BF16)], axis=1)
+
+    def ranked(flags, total):
+        out = []
+        for t in range(flags.shape[1] // LANES):
+            sums = jnp.dot(
+                flags[:, t * LANES : (t + 1) * LANES].astype(BF16), upto, preferred_element_type=F32
+            )
+            out.append(sums[:, :LANES] + total)
+            total = total + sums[:, LANES:]
+        return jnp.concatenate(out, axis=1), total
+
+    rank, total = ranked(chosen, jnp.zeros((8, LANES), F32))
+    stay_to = jnp.where(chosen[0:1] > 0.5, rank[0:1], -1.0).astype(I32)
+    slot_to = rank + (half * (sub - 1)).astype(F32)
+    leaving = (sub >= 1) & (chosen > 0.5)
+    leave_to = (jnp.sum(jnp.where(leaving, slot_to + 1.0, 0.0), axis=0, keepdims=True) - 1.0).astype(I32)
+    position = jnp.zeros((8, wide), F32)
+    for n in range(3):
+        position = jnp.where(sub == n, off_ref[n, :, 0:wide], position)
+    marks = jnp.where(sub == 0, i_row, jnp.where(sub == 1, j_row, jnp.where(sub == 2, k_row, 1)))
+    raw = lax.dot_general(
+        jnp.concatenate([thirds(position).astype(F32), marks.astype(F32)], axis=0).astype(BF16),
+        slots_of(leave_to, few), NT, preferred_element_type=F32,
+    )
+    first_position = raw[0:8] + raw[8:16] + raw[16:24]
+    first_i, first_j, first_k = (
+        jnp.clip(raw[24 + n : 25 + n].astype(I32), 0, top_value)
+        for n, top_value in enumerate((cols - 1, rows - 1, depth - 2))
+    )
+    first_real = raw[27:28] > 0.5
+
+    def words(i, j, k, target):
+        start = jnp.where(i >= LANES, span, 0) + k * level + 4 * j
+        start = start * LANES + ((iota(i.shape, 1) - i) & (LANES - 1))
+        for t in range(i.shape[1] // LANES):
+            part = start[:, t * LANES : (t + 1) * LANES]
+            target[2 * t : 2 * t + 1, :] = part
+            target[2 * t + 1 : 2 * t + 2, :] = pltpu.roll(part, half, 1)
+
+    words(first_i, first_j, first_k, first_ref)
+    words(i_row, j_row, k_row, where_ref)
+    addresses = [
+        pltpu.make_async_copy(first_ref, first_smem, asem.at[0]),
+        pltpu.make_async_copy(where_ref, where_smem, asem.at[1]),
+    ]
+    for copy in addresses:
+        copy.start()
+    stay_ref[...] = slots_of(stay_to, wide)
 
     build(1)
 
     @pl.when(top)
     def _():
         edge(nfold, cfold, rows - 1)
-        fold_out.start()
-
-    @pl.when(away)
-    def _():
-        cfold_out.start()
+
+    @pl.when(eager)
+    def _():
+        send_fold()
 
     @pl.when(jnp.logical_and(top, corner == p))
     def _():
@@ -328,7 +344,9 @@
                 n = min(LANES, depth * rows - g * LANES)
                 side[h * 3 + c, g : g + 1, 0:n] = line[:, g * LANES : g * LANES + n]
     column[...] = side[0:3].astype(BF16)
-    col_out.start()
+    @pl.when(eager)
+    def _():
+        col_out.start()
 
     def gather(source, target, count):
         def body(step, carry):
@@ -363,6 +381,13 @@
         copy.wait()
     lax.fori_loop(0, 4, gather(first_smem, first_gathered, CAP), 0)
     lax.fori_loop(0, live // half, gather(where_smem, gathered, half), 0)
+
+    @pl.when(patient)
+    def _():
+        send_rows()
+        send_fold()
+        col_out.start()
+
 
     go = iota((1, few), 1) // half + 1
     folding = (go == 3) & top

time: 20.8 us -> 20 us (0.962)
  the two profiles are of different devices: /device:TPU:6 before, /device:TPU:55 now
where the time goes in v6:
time: 20 us; the launch traced here: 19.9 us
  Pallas kernels  18.7 us (94%)
  between operations  1.29 us (6%)
    pallas_call x1, Pallas kernels, shards(): pl.pallas_call(functools.partial(kernel, dims), out_shape=jax.ShapeDtypeS...  18 us
    pallas_call x1, Pallas kernels, shards(): pl.pallas_call(functools.partial(decode, rows, cols), out_shape=(jax.Shap...  0.61 us

profile of v6, /device:TPU:55, one launch (start us, length us, event | category | flops | bytes accessed | tf_op | source)
XLA Modules:
  0.0 19.9 jit_solution(10891004443418142947)
XLA Ops:
  1.3 18.0 %advance.1.result_ref = f32[8,768]{1,0:T(8,128)S(1)} custom-call(bf16[3,75,32,256]{3,2,1,0:T(8,128)(2,1)} %vel_hbm.1, f32[3,1,768]{2,1,0:T(1,128)} %off_hbm.1, s32[3,1,768]{2,1,0:T(1,128)} %cell_hbm.1, s32[1,1]{1,0:T(1,128)S(6)} %copy.8.count_hbm, s32[1,768]{1,0:T(1,128)} %move_hbm.1), custom_call_target="tpu_custom_call" | custom-call | tf_op jit(solution)/shard_map/advance/pallas_call | solution.py:537
  19.3 0.6 %decode.1 = (f32[3,1,768]{2,1,0:T(1,128)}, s32[3,1,768]{2,1,0:T(1,128)}, s32[1,1]{1,0:T(1,128)}) custom-call(f32[8,768]{1,0:T(8,128)S(1)} %advance.1.result_ref), custom_call_target="tpu_custom_call" | custom-call | tf_op jit(solution)/shard_map/decode/pallas_call | solution.py:579

commit v7 on v6

--- a/solution.py
+++ b/solution.py
@@ -131,8 +131,8 @@
     half = LANES // 2
     few = 4 * half
     level = rows * 4
-    span = table.shape[0] // 2
-    deep = span // level
+    deep = pl.cdiv(depth, 16) * 16
+    span = deep * level
     per = LANES // rows
     groups = side.shape[1]
     r, p = lax.axis_index("lat"), lax.axis_index("lon")
@@ -237,8 +237,10 @@
     edge(nrow, cnr, 0)
     peers = 2 + 2 * (r > 0).astype(I32) + (r < n_lat - 1).astype(I32) + top.astype(I32) + away.astype(I32)
 
-    def send_rows():
+    def send_rows(*first):
         pl.semaphore_wait(barrier, peers)
+        for copy in first:
+            copy.start()
 
         @pl.when(r > 0)
         def _():
@@ -302,13 +304,15 @@
     first_real = raw[27:28] > 0.5
 
     def words(i, j, k, target):
-        start = jnp.where(i >= LANES, span, 0) + k * level + 4 * j
+        start = jnp.clip(jnp.where(i >= LANES, span, 0) + k * level + 4 * j, 0, 2 * span - level - 8)
         start = start * LANES + ((iota(i.shape, 1) - i) & (LANES - 1))
         for t in range(i.shape[1] // LANES):
             part = start[:, t * LANES : (t + 1) * LANES]
             target[2 * t : 2 * t + 1, :] = part
             target[2 * t + 1 : 2 * t + 2, :] = pltpu.roll(part, half, 1)
 
+    first_ref[...] = jnp.zeros_like(first_ref)
+    where_ref[...] = jnp.zeros_like(where_ref)
     words(first_i, first_j, first_k, first_ref)
     words(i_row, j_row, k_row, where_ref)
     addresses = [
@@ -380,13 +384,20 @@
     for copy in addresses:
         copy.wait()
     lax.fori_loop(0, 4, gather(first_smem, first_gathered, CAP), 0)
-    lax.fori_loop(0, live // half, gather(where_smem, gathered, half), 0)
+
+    later = (r % 2 == 0) & (p > 0)
+
+    def gather_rest():
+        lax.fori_loop(0, live // half, gather(where_smem, gathered, half), 0)
+
+    @pl.when(jnp.logical_not(later))
+    def _():
+        gather_rest()
 
     @pl.when(patient)
     def _():
-        send_rows()
+        send_rows(col_out)
         send_fold()
-        col_out.start()
 
 
     go = iota((1, few), 1) // half + 1
@@ -460,6 +471,10 @@
     east_out.start()
     west_out.start()
 
+    @pl.when(later)
+    def _():
+        gather_rest()
+
     corners = halo_corners(
         wide, i_row, j_row, k_row, together(gathered, wide), top, sides, nrow_in, cnr_in
     )
@@ -529,6 +544,7 @@
     deep = pl.cdiv(depth, 16) * 16
     dims = (depth, rows, cols, slots, live, lax.axis_size("lat"), lax.axis_size("lon"))
     groups = pl.cdiv(depth * rows, 8 * LANES) * 8
+    listed = pl.cdiv(2 * wide // LANES, 8) * 8
     vmem = pl.BlockSpec(memory_space=pltpu.VMEM)
     hbm = pl.BlockSpec(memory_space=pltpu.HBM)
     velocity, offsets, cells, moves = (
@@ -545,11 +561,11 @@
             pltpu.VMEM((3, 1, slots), I32),
             pltpu.VMEM((1, slots), I32),
             pltpu.VMEM((1, 1), I32),
-            pltpu.VMEM((2 * deep * rows * 4, LANES), F32),
-            pltpu.VMEM((2 * wide // LANES, LANES), I32),
-            pltpu.SMEM((2 * wide // LANES, LANES), I32),
-            pltpu.VMEM((4, LANES), I32),
-            pltpu.SMEM((4, LANES), I32),
+            pltpu.VMEM((2 * deep * rows * 4 + 8 * rows * 4, LANES), F32),
+            pltpu.VMEM((listed, LANES), I32),
+            pltpu.SMEM((listed, LANES), I32),
+            pltpu.VMEM((8, LANES), I32),
+            pltpu.SMEM((8, LANES), I32),
             pltpu.VMEM((4, wide // LANES, 8, LANES), F32),
             pltpu.VMEM((4, 2, 8, LANES), F32),
             pltpu.VMEM((wide, wide), BF16),

time: 20 us -> 19.9 us (level)
  no operation moved by 1% of the time
where the time goes in v7:
time: 19.9 us; the launch traced here: 19.8 us
  Pallas kernels  18.6 us (93%)
  between operations  1.29 us (6%)
    pallas_call x1, Pallas kernels, shards(): pl.pallas_call(functools.partial(kernel, dims), out_shape=jax.ShapeDtypeS...  17.9 us
    pallas_call x1, Pallas kernels, shards(): pl.pallas_call(functools.partial(decode, rows, cols), out_shape=(jax.Shap...  0.61 us

profile of v7, /device:TPU:55, one launch (start us, length us, event | category | flops | bytes accessed | tf_op | source)
XLA Modules:
  0.0 19.8 jit_solution(7181215266018221188)
XLA Ops:
  1.3 17.9 %advance.1.result_ref = f32[8,768]{1,0:T(8,128)S(1)} custom-call(bf16[3,75,32,256]{3,2,1,0:T(8,128)(2,1)} %vel_hbm.1, f32[3,1,768]{2,1,0:T(1,128)} %off_hbm.1, s32[3,1,768]{2,1,0:T(1,128)} %cell_hbm.1, s32[1,1]{1,0:T(1,128)S(6)} %copy.8.count_hbm, s32[1,768]{1,0:T(1,128)} %move_hbm.1), custom_call_target="tpu_custom_call" | custom-call | tf_op jit(solution)/shard_map/advance/pallas_call | solution.py:553
  19.2 0.6 %decode.1 = (f32[3,1,768]{2,1,0:T(1,128)}, s32[3,1,768]{2,1,0:T(1,128)}, s32[1,1]{1,0:T(1,128)}) custom-call(f32[8,768]{1,0:T(8,128)S(1)} %advance.1.result_ref), custom_call_target="tpu_custom_call" | custom-call | tf_op jit(solution)/shard_map/decode/pallas_call | solution.py:595

commit v8 on v7

--- a/solution.py
+++ b/solution.py
@@ -48,12 +48,8 @@
     return (1.0 - a_row) * sums[0] + a_row * sums[1]
 
 
-def halo_corners(w, i_row, j_row, k_row, inside, top, sides, nrow_in, cnr_in):
-    cols, rows = 2 * LANES, sides[0].shape[0]
-    deep = (nrow_in.shape[0] - 16) // 2
-    groups = sides[0].shape[1] // 8
-    per = LANES // rows
-    sub2 = iota((8, 2 * w), 0)
+def lookups(w, i_row, j_row, k_row, top, deep, groups, rows):
+    cols, per = 2 * LANES, LANES // rows
 
     def twice(x):
         return jnp.concatenate([x] * 2, axis=1)
@@ -70,6 +66,14 @@
     inner = base & (LANES - 1)
     at_row = hot(2 * deep, k2 + jnp.where(second, deep, 0))
     at_level = hot(LANES, k2)
+    return at_side, at_row, at_level, j2, second, inner
+
+
+def halo_corners(w, i_row, j_row, plan, inside, top, sides, nrow_in, cnr_in):
+    at_side, at_row, at_level, j2, second, inner = plan
+    rows = sides[0].shape[0]
+    deep = (nrow_in.shape[0] - 16) // 2
+    sub2 = iota((8, 2 * w), 0)
 
     eastern = jnp.zeros((8, 2 * w), F32)
     hits = [iota((rows, 2 * w), 0) == j2 + dj for dj in range(2)]
@@ -411,6 +415,7 @@
     )
     code = jnp.where(first_real, 1 + new_i + cols * (new_j + rows * first_k), 0).astype(F32)
 
+    first_plan = lookups(few, first_i, first_j, first_k, top, deep, groups, rows)
     cnr_wait = remote(cnr, cnr_in, 2, 2, r, west)
     col_out.wait_recv()
     row_out.wait_recv()
@@ -430,7 +435,7 @@
         sides.append(jnp.concatenate(lines, axis=0).T[0:rows].astype(BF16))
 
     corners = halo_corners(
-        few, first_i, first_j, first_k, together(first_gathered, few), top, sides, nrow_in, cnr_in
+        few, first_i, first_j, first_plan, together(first_gathered, few), top, sides, nrow_in, cnr_in
     )
     moved = advanced(corners, first_position)
     na, nb, nc = moved[0:1], moved[1:2], moved[2:3]
@@ -476,7 +481,7 @@
         gather_rest()
 
     corners = halo_corners(
-        wide, i_row, j_row, k_row, together(gathered, wide), top, sides, nrow_in, cnr_in
+        wide, i_row, j_row, lookups(wide, i_row, j_row, k_row, top, deep, groups, rows), together(gathered, wide), top, sides, nrow_in, cnr_in
     )
     moved = advanced(corners, position)
     code = (1 + i_row + cols * (j_row + rows * k_row)).astype(F32)

time: 19.9 us -> 19.9 us (level)
  the two profiles are of different devices: /device:TPU:55 before, /device:TPU:1 now
where the time goes in v8:
time: 19.9 us; the launch traced here: 19.6 us
  Pallas kernels  18.3 us (92%)
  between operations  1.29 us (6%)
    pallas_call x1, Pallas kernels, shards(): pl.pallas_call(functools.partial(kernel, dims), out_shape=jax.ShapeDtypeS...  17.7 us
    pallas_call x1, Pallas kernels, shards(): pl.pallas_call(functools.partial(decode, rows, cols), out_shape=(jax.Shap...  0.61 us

profile of v8, /device:TPU:1, one launch (start us, length us, event | category | flops | bytes accessed | tf_op | source)
XLA Modules:
  0.0 19.6 jit_solution(12649306974784589705)
XLA Ops:
  1.3 17.7 %advance.1.result_ref = f32[8,768]{1,0:T(8,128)S(1)} custom-call(bf16[3,75,32,256]{3,2,1,0:T(8,128)(2,1)} %vel_hbm.1, f32[3,1,768]{2,1,0:T(1,128)} %off_hbm.1, s32[3,1,768]{2,1,0:T(1,128)} %cell_hbm.1, s32[1,1]{1,0:T(1,128)S(6)} %copy.8.count_hbm, s32[1,768]{1,0:T(1,128)} %move_hbm.1), custom_call_target="tpu_custom_call" | custom-call | tf_op jit(solution)/shard_map/advance/pallas_call | solution.py:558
  19.0 0.6 %decode.1 = (f32[3,1,768]{2,1,0:T(1,128)}, s32[3,1,768]{2,1,0:T(1,128)}, s32[1,1]{1,0:T(1,128)}) custom-call(f32[8,768]{1,0:T(8,128)S(1)} %advance.1.result_ref), custom_call_target="tpu_custom_call" | custom-call | tf_op jit(solution)/shard_map/decode/pallas_call | solution.py:600
